TPU v7x, 32 devices: a whole 2x2x4 slice. The times are simulated.
32 devices in a mesh: section: 8 (over z, y), fsdp: 4 (over x, core).
Axes of the slice: x: 2, y: 2, z: 4, core: 2. Of those that a mesh axis runs over, the one named last changes fastest.
Arguments:
- source_rows: bfloat16 [3072, 4096], P(('section', 'fsdp')), may hold values from -6 to 6
- target_rows: bfloat16 [1024, 4096], P('section'), may hold values from -6 to 6
- attn_weights: bfloat16 [8, 4, 4096, 3072], P('section', None, None, 'fsdp'), may hold values from -3.76875 to 3.76875
- gains: float32 [8, 4096], P('section'), may hold values from 0.25 to 1.75
- lengths: int32 [8], P('section'), may hold values from 192 to 384
Outputs:
- source_next: bfloat16 [3072, 4096], P(('section', 'fsdp'))
- target_next: bfloat16 [1024, 4096], P('section')
Inputs may be any that keep to these rules, and one draw needn't show every extreme that they name: Keys at positions lengths[s] and beyond are padding.
All inputs are finite; a program needn't handle non-finite values.
Results may differ from a plain program's by a relative error of at most 0.015.
The roundings to bfloat16 on the way count: a program that leaves them out, or rounds other values in their place, can miss the bound.
Values may be sent and summed in bfloat16 or wider, within the bound.
No kernel may reach another device: no remote copies, remote signals or barrier semaphores. Data moves between devices by JAX's collectives and lax.ppermute only.
A program may use at most 128 MiB of HBM per device.

v0:
```python
import functools
import jax
import jax.numpy as jnp
from jax import lax
from jax.experimental import pallas as pl
from jax.experimental.pallas import tpu as pltpu
from jax.sharding import PartitionSpec as P

HEAD_DIM = 64
LOG2E = 1.4426950408889634


def shifted(value, axis, steps):
    count = lax.axis_size(axis)
    pairs = [(source, (source + steps) % count) for source in range(count)]
    return lax.ppermute(value, axis, pairs)


def rms_norm(block_rows, gain_row):
    widened = block_rows.astype(jnp.float32)
    inverse_rms = lax.rsqrt(jnp.mean(widened * widened, axis=-1, keepdims=True) + 1e-06)
    return (widened * inverse_rms * gain_row).astype(jnp.bfloat16)


def project(block_rows, weight):
    return jnp.dot(block_rows, weight, preferred_element_type=jnp.float32).astype(jnp.bfloat16)


def attend(queries, key_rows, values, length):
    query_count = queries.shape[0]
    key_count = key_rows.shape[0]
    head_count = queries.shape[1] // HEAD_DIM
    query_heads = queries.reshape(query_count, head_count, HEAD_DIM)
    key_heads = key_rows.reshape(key_count, head_count, HEAD_DIM)
    value_heads = values.reshape(key_count, head_count, HEAD_DIM)
    scores = (
        jnp.einsum("qhc,khc->hqk", query_heads, key_heads, preferred_element_type=jnp.float32)
        * 0.125
    )
    key_valid = jnp.arange(key_count, dtype=jnp.int32) < length
    scores = jnp.where(key_valid[None, None, :], scores, -1000000000.0)
    row_max = jnp.max(scores, axis=-1, keepdims=True)
    expo = jnp.exp(scores - row_max)
    soft = (expo / jnp.sum(expo, axis=-1, keepdims=True)).astype(jnp.bfloat16)
    context = jnp.einsum("hqk,khc->qhc", soft, value_heads, preferred_element_type=jnp.float32)
    return context.reshape(query_count, head_count * HEAD_DIM).astype(jnp.bfloat16)


def out_partial(context, out_weight):
    return lax.dot_general(
        context, out_weight, (((1,), (1,)), ((), ())), preferred_element_type=jnp.float32
    )


def local_general(source_rows, target_rows, attn_weights, gains, lengths):
    section_index = lax.axis_index("section")
    encoder_section = section_index < lax.axis_size("section") // 2
    weights = attn_weights[0]
    gain_row = gains[0]
    length = lengths[0]
    source_whole = lax.all_gather(source_rows, "fsdp", axis=0, tiled=True)

    def encoder_work(whole_rows, target_block):
        normed = rms_norm(whole_rows, gain_row)
        context = attend(
            project(normed, weights[0]),
            project(normed, weights[1]),
            project(normed, weights[2]),
            length,
        )
        return (out_partial(context, weights[3]), jnp.zeros(target_block.shape, jnp.float32))

    def decoder_work(whole_rows, target_block):
        normed = rms_norm(target_block, gain_row)
        context = attend(
            project(normed, weights[0]),
            project(whole_rows, weights[1]),
            project(whole_rows, weights[2]),
            length,
        )
        return (jnp.zeros(whole_rows.shape, jnp.float32), out_partial(context, weights[3]))

    source_terms, target_terms = lax.cond(
        encoder_section, encoder_work, decoder_work, source_whole, target_rows
    )
    source_sum = lax.psum_scatter(
        source_terms.astype(jnp.bfloat16), "fsdp", scatter_dimension=0, tiled=True
    ).astype(jnp.float32)
    source_new = (source_rows.astype(jnp.float32) + source_sum).astype(jnp.bfloat16)
    target_sum = lax.psum(target_terms.astype(jnp.bfloat16), "fsdp").astype(jnp.float32)
    target_new = (target_rows.astype(jnp.float32) + target_sum).astype(jnp.bfloat16)
    source_next, target_next = shifted((source_new, target_new), "section", 1)
    return (source_next, target_next)


PARAMS = pltpu.CompilerParams(vmem_limit_bytes=24 * 1024 * 1024)
PARTS = 4
WEIGHT_PARAMS = pltpu.CompilerParams(vmem_limit_bytes=42 * 1024 * 1024)


def norm_kernel(ids, x_ref, gain_ref, *outs):
    piece = outs[1].shape[0]

    def put(value):
        outs[0][...] = value
        for index, out in enumerate(outs[1:]):
            out[...] = value[index * piece : (index + 1) * piece]

    @pl.when(ids[0] == 1)
    def _():
        put(rms_norm(x_ref[...], gain_ref[...]))

    @pl.when(ids[0] == 0)
    def _():
        put(x_ref[...])


def norm_rows(ids, rows, gains, chunks):
    count, width = rows.shape
    shapes = [(count, width)] + [(count // chunks, width)] * chunks
    return pl.pallas_call(
        norm_kernel,
        grid_spec=pltpu.PrefetchScalarGridSpec(
            num_scalar_prefetch=1,
            grid=(1,),
            in_specs=[
                pl.BlockSpec((count, width), lambda i, s: (0, 0)),
                pl.BlockSpec((1, width), lambda i, s: (0, 0)),
            ],
            out_specs=[pl.BlockSpec(shape, lambda i, s: (0, 0)) for shape in shapes],
        ),
        out_shape=[jax.ShapeDtypeStruct(shape, jnp.bfloat16) for shape in shapes],
        compiler_params=PARAMS,
        cost_estimate=pl.CostEstimate(
            flops=count * width * 200, bytes_accessed=count * width * 4, transcendentals=0
        ),
        name="norm_rows",
    )(ids, rows, gains)


def qkv_kernel(n_pieces, n_query, ids, *refs):
    pieces = refs[:n_pieces]
    sibling_pieces = refs[n_pieces : 2 * n_pieces]
    y_ref, gain_ref, w_ref = refs[2 * n_pieces : 2 * n_pieces + 3]
    o_ref, x_all, y_all = refs[-3:]
    step = pl.program_id(0)
    encoder, core = ids[0], ids[2]
    rows = x_all.shape[0] // 2
    piece = rows // n_pieces

    @pl.when(step == 0)
    def _():
        for index in range(n_pieces):
            mine = pl.multiple_of(core * rows + index * piece, piece)
            other = pl.multiple_of((1 - core) * rows + index * piece, piece)
            x_all[pl.ds(mine, piece), :] = pieces[index][...]
            x_all[pl.ds(other, piece), :] = sibling_pieces[index][...]

        @pl.when(encoder == 0)
        def _():
            y_all[...] = rms_norm(y_ref[...], gain_ref[...])

    from_target = jnp.logical_and(encoder == 0, step < n_query)

    @pl.when(jnp.logical_not(from_target))
    def _():
        o_ref[...] = jnp.dot(
            x_all[...], w_ref[...], preferred_element_type=jnp.float32
        ).astype(jnp.bfloat16)

    @pl.when(from_target)
    def _():
        queries = jnp.dot(
            y_all[...], w_ref[...], preferred_element_type=jnp.float32
        ).astype(jnp.bfloat16)
        half = queries.shape[0] // 2
        o_ref[...] = jnp.zeros_like(o_ref)
        o_ref[0:half, :] = queries[:half]
        o_ref[rows : rows + half, :] = queries[half:]


def qkv_rows(ids, pieces, sibling_pieces, target_rows, gains, attn_weights, slot_index, into):
    n_pieces = len(pieces)
    rows = sum(p.shape[0] for p in pieces)
    width = pieces[0].shape[1]
    inner = attn_weights.shape[3]
    tile = 256
    per = inner // tile
    part = target_rows.shape[0] // 2
    in_specs = [pl.BlockSpec(p.shape, lambda i, s: (0, 0)) for p in pieces + sibling_pieces]
    in_specs += [
        pl.BlockSpec((part, width), lambda i, s: (s[slot_index], 0)),
        pl.BlockSpec((1, width), lambda i, s: (0, 0)),
        pl.BlockSpec((None, None, width, tile), lambda i, s: (0, i // per, 0, i % per)),
    ]
    operands = [ids, *pieces, *sibling_pieces, target_rows, gains, attn_weights]
    aliases = {}
    if into is not None:
        in_specs.append(pl.BlockSpec(memory_space=pl.ANY))
        aliases = {len(operands): 0}
        operands.append(into)
    return pl.pallas_call(
        functools.partial(qkv_kernel, n_pieces, per),
        grid_spec=pltpu.PrefetchScalarGridSpec(
            num_scalar_prefetch=1,
            grid=(3 * per,),
            in_specs=in_specs,
            out_specs=pl.BlockSpec((2 * rows, tile), lambda i, s: (s[slot_index], i)),
            scratch_shapes=[
                pltpu.VMEM((2 * rows, width), jnp.bfloat16),
                pltpu.VMEM((part, width), jnp.bfloat16),
            ],
        ),
        out_shape=jax.ShapeDtypeStruct((4 * rows, 3 * inner), jnp.bfloat16),
        input_output_aliases=aliases,
        cost_estimate=pl.CostEstimate(
            flops=2 * 2 * rows * width * 3 * inner,
            bytes_accessed=2 * width * 3 * inner,
            transcendentals=0,
        ),
        compiler_params=WEIGHT_PARAMS,
        name="qkv_rows",
    )(*operands)


def attend_kernel(ids, q_ref, k_ref, v_ref, ctx):
    length = ids[4]
    rows, inner = q_ref.shape
    count = k_ref.shape[0]
    valid = lax.broadcasted_iota(jnp.int32, (rows, count), 1) < length
    low = lax.broadcasted_iota(jnp.int32, (rows, 2 * HEAD_DIM), 1) < HEAD_DIM
    for pair in range(inner // (2 * HEAD_DIM)):
        lanes = slice(pair * 2 * HEAD_DIM, (pair + 1) * 2 * HEAD_DIM)
        q_pair = q_ref[:, lanes]
        k_pair = k_ref[:, lanes]
        v_pair = v_ref[:, lanes]
        parts = []
        for head in range(2):
            mask = low if head == 0 else jnp.logical_not(low)
            q_head = jnp.where(mask, q_pair, jnp.zeros_like(q_pair))
            scores = lax.dot_general(
                q_head, k_pair, (((1,), (1,)), ((), ())), preferred_element_type=jnp.float32
            )
            scores = jnp.where(valid, scores, -8000000000.0)
            row_max = jnp.max(scores, axis=-1, keepdims=True)
            expo = jnp.exp2((scores - row_max) * (0.125 * LOG2E))
            total = jnp.sum(expo, axis=-1, keepdims=True)
            soft = (expo * (1.0 / total)).astype(jnp.bfloat16)
            parts.append(jnp.dot(soft, v_pair, preferred_element_type=jnp.float32))
        ctx[:, lanes] = jnp.where(low, parts[0], parts[1]).astype(jnp.bfloat16)


def attend_rows(ids, qkv, inner):
    total = qkv.shape[0]
    return pl.pallas_call(
        attend_kernel,
        grid_spec=pltpu.PrefetchScalarGridSpec(
            num_scalar_prefetch=1,
            grid=(1,),
            in_specs=[
                pl.BlockSpec((total, inner), lambda i, s: (0, 0)),
                pl.BlockSpec((total, inner), lambda i, s: (0, 1)),
                pl.BlockSpec((total, inner), lambda i, s: (0, 2)),
            ],
            out_specs=pl.BlockSpec((total, inner), lambda i, s: (0, 0)),
        ),
        out_shape=jax.ShapeDtypeStruct((total, inner), jnp.bfloat16),
        compiler_params=PARAMS,
        cost_estimate=pl.CostEstimate(
            flops=40 * total * total * inner, bytes_accessed=8 * total * inner, transcendentals=0
        ),
        name="attend_rows",
    )(ids, qkv, qkv, qkv)


def out_kernel(ids, c0, c1, c2, c3, w_ref, keep_ref, send_ref):
    context = jnp.concatenate([c[...] for c in (c0, c1, c2, c3)], axis=0)
    terms = out_partial(context, w_ref[...]).astype(jnp.bfloat16)
    half = terms.shape[0] // 2
    keep_ref[...] = terms[:half]
    send_ref[...] = terms[half:]


def out_chunk(ids, context, attn_weights, chunk, parts):
    total, inner = context.shape
    span = attn_weights.shape[2] // parts
    tile = span // 2

    def rows_spec(slot):
        return pl.BlockSpec((total // 4, inner), lambda i, s: (s[slot], 0))

    half = jax.ShapeDtypeStruct((total // 2, span), jnp.bfloat16)
    return pl.pallas_call(
        out_kernel,
        grid_spec=pltpu.PrefetchScalarGridSpec(
            num_scalar_prefetch=1,
            grid=(2,),
            in_specs=[
                rows_spec(5),
                rows_spec(6),
                rows_spec(7),
                rows_spec(8),
                pl.BlockSpec((None, None, tile, inner), lambda i, s: (0, 3, 2 * chunk + i, 0)),
            ],
            out_specs=[pl.BlockSpec((total // 2, tile), lambda i, s: (0, i))] * 2,
        ),
        out_shape=[half, half],
        compiler_params=WEIGHT_PARAMS,
        cost_estimate=pl.CostEstimate(
            flops=2 * total * span * inner, bytes_accessed=2 * span * inner, transcendentals=0
        ),
        name="out_chunk",
    )(ids, context, context, context, context, attn_weights)


def small_call(kernel, ids, operands, blocks, out_shape):
    def spec(shape, index):
        row, column = index
        if row == "here":
            return pl.BlockSpec(shape, lambda i, s: (s[5], column))
        return pl.BlockSpec(shape, lambda i, s: (row, column))

    return pl.pallas_call(
        kernel,
        grid_spec=pltpu.PrefetchScalarGridSpec(
            num_scalar_prefetch=1,
            grid=(1,),
            in_specs=[spec(*b) for b in blocks],
            out_specs=pl.BlockSpec(out_shape, lambda i, s: (0, 0)),
        ),
        out_shape=jax.ShapeDtypeStruct(out_shape, jnp.bfloat16),
        compiler_params=PARAMS,
        cost_estimate=pl.CostEstimate(
            flops=out_shape[0] * out_shape[1] * 200,
            bytes_accessed=out_shape[0] * out_shape[1] * 8,
            transcendentals=0,
        ),
    )(ids, *operands)


def pair_kernel(ids, keep_ref, taken_ref, o_ref):
    o_ref[...] = (
        keep_ref[...].astype(jnp.float32) + taken_ref[...].astype(jnp.float32)
    ).astype(jnp.bfloat16)


def final_kernel(ids, keep_ref, taken_ref, crossed_ref, source_ref, target_ref, o_ref):
    f32 = jnp.float32
    total = keep_ref[...].astype(f32) + taken_ref[...].astype(f32) + crossed_ref[...].astype(f32)
    o_ref[...] = (source_ref[...].astype(f32) + total).astype(jnp.bfloat16)

    @pl.when(ids[0] == 0)
    def _():
        part = target_ref.shape[0]
        o_ref[0:part, :] = (target_ref[...].astype(f32) + total[:part]).astype(jnp.bfloat16)


def target_kernel(ids, *refs):
    early_ref, o_ref = refs[-2:]

    @pl.when(ids[9] == 1)
    def _():
        o_ref[...] = early_ref[...]

    @pl.when(ids[9] == 0)
    def _():
        column = 0
        for group in range(len(refs[:-2]) // 4):
            blocks = refs[4 * group : 4 * group + 4]
            piece, span = blocks[0].shape
            for slot, ref in zip((5, 7, 6, 8), blocks):
                rows = pl.ds(pl.multiple_of(ids[slot] * piece, piece), piece)
                o_ref[rows, column : column + span] = ref[...]
            column += span


def source_kernel(ids, *refs):
    moved, early_ref, o_ref = refs[:-2], refs[-2], refs[-1]
    span = moved[0].shape[1]

    @pl.when(ids[9] == 1)
    def _():
        for index, ref in enumerate(moved):
            o_ref[:, index * span : (index + 1) * span] = ref[...]

    @pl.when(ids[9] == 0)
    def _():
        o_ref[...] = early_ref[...]


def local_pairs(chunks, source_rows, target_rows, attn_weights, gains, lengths):
    n_section = lax.axis_size("section")
    n_encoder = n_section // 2
    section = lax.axis_index("section")
    here = lax.axis_index("fsdp")
    is_encoder = section < n_encoder
    from_encoder = jnp.logical_and(section >= 1, section <= n_encoder)
    ids = jnp.stack(
        [
            is_encoder.astype(jnp.int32),
            here // 2,
            here % 2,
            1 - here // 2,
            lengths[0],
            here,
            here ^ 2,
            here ^ 1,
            here ^ 3,
            from_encoder.astype(jnp.int32),
        ]
    ).astype(jnp.int32)
    own, width = source_rows.shape
    piece = own // chunks
    block = (piece, width)

    def to_sibling(value):
        return lax.ppermute(value, "fsdp", [(0, 1), (1, 0), (2, 3), (3, 2)])

    def across(value):
        return lax.ppermute(value, "fsdp", [(0, 2), (2, 0), (1, 3), (3, 1)])

    def onward(value, first, last):
        pairs = [(s, (s + 1) % n_section) for s in range(first, last)]
        return lax.ppermute(value, "section", pairs)

    normed, *pieces = norm_rows(ids, source_rows, gains, chunks)
    near = to_sibling(normed)
    remote = []
    for i in range(chunks):
        remote.append(across(pieces[i]))
    early_source = onward(source_rows, n_encoder, n_section)
    early_target = onward(target_rows, 0, n_encoder)
    qkv = qkv_rows(ids, [normed], [near], target_rows, gains, attn_weights, 1, None)
    remote_near = []
    for i in range(chunks):
        remote_near.append(to_sibling(remote[i]))
    qkv = qkv_rows(ids, remote, remote_near, target_rows, gains, attn_weights, 3, qkv)

    context = attend_rows(ids, qkv, attn_weights.shape[3])
    span = width // PARTS
    part = target_rows.shape[0] // 4
    block = (own, span)
    moved = []
    for i in range(PARTS):
        keep, send = out_chunk(ids, context, attn_weights, i, PARTS)
        taken = to_sibling(send)
        for_other = small_call(
            pair_kernel, ids,
            [keep, taken], [(block, (1, 0)), (block, (1, 0))], block,
        )
        crossed = across(for_other)
        new = small_call(
            final_kernel, ids,
            [keep, taken, crossed, source_rows, target_rows],
            [(block, (0, 0))] * 3 + [(block, (0, i)), ((part, span), ("here", i))],
            block,
        )
        moved.append(onward(new, 0, n_section))

    groups = []
    for members in (moved[:-1], moved[-1:]):
        mine = jnp.concatenate([m[:part] for m in members], axis=1)
        other = across(mine)
        sibling = to_sibling(mine)
        diagonal = to_sibling(other)
        groups += [mine, sibling, other, diagonal]
    source_next = small_call(
        source_kernel, ids,
        [*moved, early_source],
        [(block, (0, 0))] * PARTS + [((own, width), (0, 0))],
        (own, width),
    )
    target_next = small_call(
        target_kernel, ids,
        [*groups, early_target],
        [(g.shape, (0, 0)) for g in groups] + [(target_rows.shape, (0, 0))],
        target_rows.shape,
    )
    return (source_next, target_next)


def solution(mesh):
    in_specs = (
        P(("section", "fsdp"), None),
        P("section", None),
        P("section", None, None, "fsdp"),
        P("section", None),
        P("section"),
    )
    out_specs = (P(("section", "fsdp"), None), P("section", None))

    def shape_test(source_rows, target_rows, attn_weights, gains, lengths):
        n_section, n_fsdp = mesh.shape["section"], mesh.shape["fsdp"]
        own = source_rows.shape[0] // (n_section * n_fsdp)
        part = target_rows.shape[0] // (n_section * n_fsdp)
        paired = (
            n_fsdp == 4
            and part * n_section * n_fsdp == target_rows.shape[0]
            and part % 16 == 0
            and own % part == 0
            and attn_weights.shape[3] // n_fsdp % 256 == 0
            and attn_weights.shape[2] % (256 * PARTS) == 0
        )
        return own // part if paired else 0

    def mapped(body):
        return jax.shard_map(
            body, mesh=mesh, in_specs=in_specs, out_specs=out_specs, check_vma=False
        )

    def run(*arrays):
        chunks = shape_test(*arrays)
        if not chunks:
            return mapped(local_general)(*arrays)
        step = mapped(functools.partial(local_pairs, chunks))
        return step(*arrays)

    return run
```

profile of v0, /device:TPU:0, one launch (start us, length us, event | category | flops | bytes accessed | tf_op | source)
XLA Modules:
  0.0 130.9 jit_solution(2814259927092202307)
XLA Ops:
  1.3 0.1 stack.47.ids
  1.4 1.1 copy-done.2
  2.5 0.7 copy-done.4
  3.2 1.0 norm_rows.1
  4.3 0.6 collective-permute-start.6
  4.8 2.6 %collective-permute-start = (bf16[32,4096]{1,0:T(8,128)(2,1)S(1)}, bf16[32,4096]{1,0:T(8,128)(2,1)S(1)}, u32[]{:S(2)}, u32[]{:S(2)}) collective-permute-start(bf16[32,4096]{1,0:T(8,128)(2,1)S(1)} %get-tuple-element.14), channel_id=1, source_target_pairs={{0,2},{2,0},{1,3},{3,1},{4,6},{6,4},{5,7},{7,5},{8,10},{10,8},{9,1... | collective-permute-start | bytes 786440 | tf_op jit(solution)/shard_map/ppermute | solution.py:420
  7.4 0.1 collective-permute-start.1
  7.5 1.9 %collective-permute-start.2 = (bf16[32,4096]{1,0:T(8,128)(2,1)S(1)}, bf16[32,4096]{1,0:T(8,128)(2,1)S(1)}, u32[]{:S(2)}, u32[]{:S(2)}) collective-permute-start(bf16[32,4096]{1,0:T(8,128)(2,1)S(1)} %get-tuple-element.16), channel_id=1, source_target_pairs={{0,2},{2,0},{1,3},{3,1},{4,6},{6,4},{5,7},{7,5},{8,10},{10,8},{9,1... | collective-permute-start | bytes 786440 | tf_op jit(solution)/shard_map/ppermute | solution.py:420
  9.4 5.1 %collective-permute-done.refs_0_ = bf16[32,4096]{1,0:T(8,128)(2,1)S(1)} collective-permute-done((bf16[32,4096]{1,0:T(8,128)(2,1)S(1)}, bf16[32,4096]{1,0:T(8,128)(2,1)S(1)}, u32[]{:S(2)}, u32[]{:S(2)}) %collective-permute-start) | collective-permute-done | bytes 262176 | tf_op jit(solution)/shard_map/ppermute | solution.py:420
  14.6 5.6 %collective-permute-done.1.refs_1_ = bf16[32,4096]{1,0:T(8,128)(2,1)S(1)} collective-permute-done((bf16[32,4096]{1,0:T(8,128)(2,1)S(1)}, bf16[32,4096]{1,0:T(8,128)(2,1)S(1)}, u32[]{:S(2)}, u32[]{:S(2)}) %collective-permute-start.1) | collective-permute-done | bytes 262176 | tf_op jit(solution)/shard_map/ppermute | solution.py:420
  20.2 5.4 %collective-permute-done.2.refs_2_ = bf16[32,4096]{1,0:T(8,128)(2,1)S(1)} collective-permute-done((bf16[32,4096]{1,0:T(8,128)(2,1)S(1)}, bf16[32,4096]{1,0:T(8,128)(2,1)S(1)}, u32[]{:S(2)}, u32[]{:S(2)}) %collective-permute-start.2) | collective-permute-done | bytes 262176 | tf_op jit(solution)/shard_map/ppermute | solution.py:420
  25.5 0.0 collective-permute-start.5
  25.5 0.0 collective-permute-done.6.refs_1_
  25.5 1.2 copy-done
  26.8 0.7 copy-done.5
  27.5 11.9 %qkv_rows.2.refs_9_ = bf16[384,2304]{1,0:T(8,128)(2,1)S(1)} custom-call(s32[10]{0:T(128)S(1)} %stack.47.ids, bf16[96,4096]{1,0:T(8,128)(2,1)S(1)} %get-tuple-element.17.refs_0_, bf16[96,4096]{1,0:T(8,128)(2,1)S(1)} %collective-permute-done.6.refs_1_, bf16[128,4096]{1,0:T(8,128)(2,1)S(1)} %copy-done, f32[1,4096]{1,0:T(1,128)S(1)} %copy-done.5, ...), custom_call_target="tpu_custom_call" | custom-call | flops 3623878656 | bytes 18874368 | tf_op jit(solution)/shard_map/qkv_rows/pallas_call | solution.py:202
  39.4 0.0 collective-permute-done.3.refs_3_
  39.4 0.0 collective-permute-done.4.refs_4_
  39.5 11.9 %qkv_rows.3.q_ref.k_ref.v_ref = bf16[384,2304]{1,0:T(8,128)(2,1)S(1)} custom-call(s32[10]{0:T(128)S(1)} %stack.47.ids, bf16[32,4096]{1,0:T(8,128)(2,1)S(1)} %collective-permute-done.refs_0_, bf16[32,4096]{1,0:T(8,128)(2,1)S(1)} %collective-permute-done.1.refs_1_, ...), custom_call_target="tpu_custom_call", output_to_operand_aliasing={{}: (10, {})} | custom-call | flops 3623878656 | bytes 18874368 | tf_op jit(solution)/shard_map/qkv_rows/pallas_call | solution.py:202
  51.4 6.1 %attend_rows.1.c0.c1.c2.c3 = bf16[384,768]{1,0:T(8,128)(2,1)S(1)} custom-call(s32[10]{0:T(128)S(1)} %stack.47.ids, bf16[384,2304]{1,0:T(8,128)(2,1)S(1)} %qkv_rows.3.q_ref.k_ref.v_ref, bf16[384,2304]{1,0:T(8,128)(2,1)S(1)} %qkv_rows.3.q_ref.k_ref.v_ref, bf16[384,2304]{1,0:T(8,128)(2,1)S(1)} %qkv_rows.3.q_ref.k_ref.v_ref), custom_call_target="tpu_custom_call" | custom-call | flops 4529848320 | bytes 2359296 | tf_op jit(solution)/shard_map/attend_rows/pallas_call | solution.py:255
  57.5 2.8 %out_chunk.6 = (bf16[192,1024]{1,0:T(8,128)(2,1)S(1)}, bf16[192,1024]{1,0:T(8,128)(2,1)S(1)}) custom-call(s32[10]{0:T(128)S(1)} %stack.47.ids, bf16[384,768]{1,0:T(8,128)(2,1)S(1)} %attend_rows.1.c0.c1.c2.c3, bf16[384,768]{1,0:T(8,128)(2,1)S(1)} %attend_rows.1.c0.c1.c2.c3, bf16[384,768]{1,0:T(8,128)(2,1)S(1)} %attend_rows.1.c0.c1.c2.c3, ...), custom_call_target="tpu_custom_call" | custom-call | flops 603979776 | bytes 1572864 | tf_op jit(solution)/shard_map/out_chunk/pallas_call | solution.py:293
  60.3 2.8 %out_chunk.5 = (bf16[192,1024]{1,0:T(8,128)(2,1)S(1)}, bf16[192,1024]{1,0:T(8,128)(2,1)S(1)}) custom-call(s32[10]{0:T(128)S(1)} %stack.47.ids, bf16[384,768]{1,0:T(8,128)(2,1)S(1)} %attend_rows.1.c0.c1.c2.c3, bf16[384,768]{1,0:T(8,128)(2,1)S(1)} %attend_rows.1.c0.c1.c2.c3, bf16[384,768]{1,0:T(8,128)(2,1)S(1)} %attend_rows.1.c0.c1.c2.c3, ...), custom_call_target="tpu_custom_call" | custom-call | flops 603979776 | bytes 1572864 | tf_op jit(solution)/shard_map/out_chunk/pallas_call | solution.py:293
  63.0 0.6 collective-permute-start.13
  63.6 0.1 collective-permute-start.10
  63.7 2.7 %out_chunk.4 = (bf16[192,1024]{1,0:T(8,128)(2,1)S(1)}, bf16[192,1024]{1,0:T(8,128)(2,1)S(1)}) custom-call(s32[10]{0:T(128)S(1)} %stack.47.ids, bf16[384,768]{1,0:T(8,128)(2,1)S(1)} %attend_rows.1.c0.c1.c2.c3, bf16[384,768]{1,0:T(8,128)(2,1)S(1)} %attend_rows.1.c0.c1.c2.c3, bf16[384,768]{1,0:T(8,128)(2,1)S(1)} %attend_rows.1.c0.c1.c2.c3, ...), custom_call_target="tpu_custom_call" | custom-call | flops 603979776 | bytes 1572864 | tf_op jit(solution)/shard_map/out_chunk/pallas_call | solution.py:293
  66.4 0.5 collective-permute-start.7
  66.9 2.8 %out_chunk.7 = (bf16[192,1024]{1,0:T(8,128)(2,1)S(1)}, bf16[192,1024]{1,0:T(8,128)(2,1)S(1)}) custom-call(s32[10]{0:T(128)S(1)} %stack.47.ids, bf16[384,768]{1,0:T(8,128)(2,1)S(1)} %attend_rows.1.c0.c1.c2.c3, bf16[384,768]{1,0:T(8,128)(2,1)S(1)} %attend_rows.1.c0.c1.c2.c3, bf16[384,768]{1,0:T(8,128)(2,1)S(1)} %attend_rows.1.c0.c1.c2.c3, ...), custom_call_target="tpu_custom_call" | custom-call | flops 603979776 | bytes 1572864 | tf_op jit(solution)/shard_map/out_chunk/pallas_call | solution.py:293
  69.7 0.0 copy-start.3
  69.7 0.1 collective-permute-start.16
  69.9 0.6 shard_map.72
  70.5 1.8 %collective-permute-start.14 = (bf16[96,1024]{1,0:T(8,128)(2,1)S(1)}, bf16[96,1024]{1,0:T(8,128)(2,1)S(1)}, u32[]{:S(2)}, u32[]{:S(2)}) collective-permute-start(bf16[96,1024]{1,0:T(8,128)(2,1)S(1)} %shard_map.72), channel_id=1, source_target_pairs={{0,2},{2,0},{1,3},{3,1},{4,6},{6,4},{5,7},{7,5},{8,10},{10,8},{9,1... | collective-permute-start | bytes 589832 | tf_op jit(solution)/shard_map/ppermute | solution.py:420
  72.3 0.0 collective-permute-done.10.taken_ref
  72.3 0.6 shard_map.70
  72.9 0.3 collective-permute-start.11
  73.2 0.0 collective-permute-done.7.taken_ref
  73.2 0.6 shard_map.68
  73.8 1.8 %collective-permute-start.8 = (bf16[96,1024]{1,0:T(8,128)(2,1)S(1)}, bf16[96,1024]{1,0:T(8,128)(2,1)S(1)}, u32[]{:S(2)}, u32[]{:S(2)}) collective-permute-start(bf16[96,1024]{1,0:T(8,128)(2,1)S(1)} %shard_map.68), channel_id=1, source_target_pairs={{0,2},{2,0},{1,3},{3,1},{4,6},{6,4},{5,7},{7,5},{8,10},{10,8},{9,1... | collective-permute-start | bytes 589832 | tf_op jit(solution)/shard_map/ppermute | solution.py:420
  75.6 3.5 %collective-permute-start.26 = (bf16[128,4096]{1,0:T(8,128)(2,1)S(1)}, bf16[128,4096]{1,0:T(8,128)(2,1)S(1)}, u32[]{:S(2)}, u32[]{:S(2)}) collective-permute-start(bf16[128,4096]{1,0:T(8,128)(2,1)S(1)} %copy-done.1), channel_id=1, source_target_pairs={{0,4},{4,8},{8,12},{12,16},{1,5},{5,9},{9,13},{13,17},{2,6},{6,10}... | collective-permute-start | bytes 3145736 | tf_op jit(solution)/shard_map/ppermute | solution.py:424
  79.1 0.6 shard_map.73
  79.8 1.5 %collective-permute-start.15 = (bf16[96,1024]{1,0:T(8,128)(2,1)S(1)}, bf16[96,1024]{1,0:T(8,128)(2,1)S(1)}, u32[]{:S(2)}, u32[]{:S(2)}) collective-permute-start(bf16[96,1024]{1,0:T(8,128)(2,1)S(1)} %shard_map.73), channel_id=1, source_target_pairs={{0,4},{4,8},{8,12},{12,16},{16,20},{20,24},{24,28},{28,0},{1,5},{5... | collective-permute-start | bytes 589832 | tf_op jit(solution)/shard_map/ppermute | solution.py:424
  81.3 1.2 collective-permute-done.11.crossed_ref
  82.5 0.6 shard_map.71
  83.2 1.8 %collective-permute-start.12 = (bf16[96,1024]{1,0:T(8,128)(2,1)S(1)}, bf16[96,1024]{1,0:T(8,128)(2,1)S(1)}, u32[]{:S(2)}, u32[]{:S(2)}) collective-permute-start(bf16[96,1024]{1,0:T(8,128)(2,1)S(1)} %shard_map.71), channel_id=1, source_target_pairs={{0,4},{4,8},{8,12},{12,16},{16,20},{20,24},{24,28},{28,0},{1,5},{5... | collective-permute-start | bytes 589832 | tf_op jit(solution)/shard_map/ppermute | solution.py:424
  85.0 1.2 collective-permute-done.8.crossed_ref
  86.2 0.6 shard_map.69
  86.9 1.8 %collective-permute-start.9 = (bf16[96,1024]{1,0:T(8,128)(2,1)S(1)}, bf16[96,1024]{1,0:T(8,128)(2,1)S(1)}, u32[]{:S(2)}, u32[]{:S(2)}) collective-permute-start(bf16[96,1024]{1,0:T(8,128)(2,1)S(1)} %shard_map.69), channel_id=1, source_target_pairs={{0,4},{4,8},{8,12},{12,16},{16,20},{20,24},{24,28},{28,0},{1,5},{5... | collective-permute-start | bytes 589832 | tf_op jit(solution)/shard_map/ppermute | solution.py:424
  88.7 1.3 collective-permute-start.19
  90.0 0.6 shard_map.74
  90.6 16.2 %collective-permute-done.15.refs_2_ = bf16[96,1024]{1,0:T(8,128)(2,1)S(1)} collective-permute-done((bf16[96,1024]{1,0:T(8,128)(2,1)S(1)}, bf16[96,1024]{1,0:T(8,128)(2,1)S(1)}, u32[]{:S(2)}, u32[]{:S(2)}) %collective-permute-start.15) | collective-permute-done | bytes 196640 | tf_op jit(solution)/shard_map/ppermute | solution.py:424
  106.8 0.5 collective-permute-start.17
  107.3 3.7 %collective-permute-done.12.refs_1_ = bf16[96,1024]{1,0:T(8,128)(2,1)S(1)} collective-permute-done((bf16[96,1024]{1,0:T(8,128)(2,1)S(1)}, bf16[96,1024]{1,0:T(8,128)(2,1)S(1)}, u32[]{:S(2)}, u32[]{:S(2)}) %collective-permute-start.12) | collective-permute-done | bytes 196640 | tf_op jit(solution)/shard_map/ppermute | solution.py:424
  111.0 2.8 %collective-permute-done.9.refs_0_ = bf16[96,1024]{1,0:T(8,128)(2,1)S(1)} collective-permute-done((bf16[96,1024]{1,0:T(8,128)(2,1)S(1)}, bf16[96,1024]{1,0:T(8,128)(2,1)S(1)}, u32[]{:S(2)}, u32[]{:S(2)}) %collective-permute-start.9) | collective-permute-done | bytes 196640 | tf_op jit(solution)/shard_map/ppermute | solution.py:424
  113.9 0.6 collective-permute-start.21
  114.5 0.0 collective-permute-done.17.crossed_ref
  114.5 0.6 shard_map.75
  115.1 2.5 %collective-permute-start.18 = (bf16[96,1024]{1,0:T(8,128)(2,1)S(1)}, bf16[96,1024]{1,0:T(8,128)(2,1)S(1)}, u32[]{:S(2)}, u32[]{:S(2)}) collective-permute-start(bf16[96,1024]{1,0:T(8,128)(2,1)S(1)} %shard_map.75), channel_id=1, source_target_pairs={{0,4},{4,8},{8,12},{12,16},{16,20},{20,24},{24,28},{28,0},{1,5},{5... | collective-permute-start | bytes 589832 | tf_op jit(solution)/shard_map/ppermute | solution.py:424
  117.7 2.0 %collective-permute-done.21.refs_2_ = bf16[32,3072]{1,0:T(8,128)(2,1)S(1)} collective-permute-done((bf16[32,3072]{1,0:T(8,128)(2,1)S(1)}, bf16[32,3072]{1,0:T(8,128)(2,1)S(1)}, u32[]{:S(2)}, u32[]{:S(2)}) %collective-permute-start.21) | collective-permute-done | bytes 196640 | tf_op jit(solution)/shard_map/ppermute | solution.py:420
  119.6 0.0 collective-permute-start.22
  119.6 3.9 %collective-permute-done.18.refs_3_ = bf16[96,1024]{1,0:T(8,128)(2,1)S(1)} collective-permute-done((bf16[96,1024]{1,0:T(8,128)(2,1)S(1)}, bf16[96,1024]{1,0:T(8,128)(2,1)S(1)}, u32[]{:S(2)}, u32[]{:S(2)}) %collective-permute-start.18) | collective-permute-done | bytes 196640 | tf_op jit(solution)/shard_map/ppermute | solution.py:424
  123.5 1.5 %collective-permute-start.24 = (bf16[32,1024]{1,0:T(8,128)(2,1)S(1)}, bf16[32,1024]{1,0:T(8,128)(2,1)S(1)}, u32[]{:S(2)}, u32[]{:S(2)}) collective-permute-start(bf16[32,1024]{1,0:T(8,128)(2,1)S(1)} %slice.19.refs_4_), channel_id=1, source_target_pairs={{0,2},{2,0},{1,3},{3,1},{4,6},{6,4},{5,7},{7,5},{8,10},{10,8},{9,1... | collective-permute-start | bytes 196616 | tf_op jit(solution)/shard_map/ppermute | solution.py:420
  125.1 2.8 %collective-permute-done.24.refs_6_ = bf16[32,1024]{1,0:T(8,128)(2,1)S(1)} collective-permute-done((bf16[32,1024]{1,0:T(8,128)(2,1)S(1)}, bf16[32,1024]{1,0:T(8,128)(2,1)S(1)}, u32[]{:S(2)}, u32[]{:S(2)}) %collective-permute-start.24) | collective-permute-done | bytes 65568 | tf_op jit(solution)/shard_map/ppermute | solution.py:420
  127.8 0.0 collective-permute-start.25
  127.8 1.5 %shard_map.76 = bf16[96,4096]{1,0:T(8,128)(2,1)} custom-call(s32[10]{0:T(128)S(1)} %stack.47.ids, bf16[96,1024]{1,0:T(8,128)(2,1)S(1)} %collective-permute-done.9.refs_0_, bf16[96,1024]{1,0:T(8,128)(2,1)S(1)} %collective-permute-done.12.refs_1_, bf16[96,1024]{1,0:T(8,128)(2,1)S(1)} %collective-permute-done.15.refs_2_, ...), custom_call_target="tpu_custom_call" | custom-call | flops 78643200 | bytes 3145728 | tf_op jit(solution)/shard_map/pallas_call | solution.py:323
  129.3 1.6 %shard_map.77 = bf16[128,4096]{1,0:T(8,128)(2,1)} custom-call(s32[10]{0:T(128)S(1)} %stack.47.ids, bf16[32,3072]{1,0:T(8,128)(2,1)S(1)} %pad_maximum_fusion.refs_0_, bf16[32,3072]{1,0:T(8,128)(2,1)S(1)} %collective-permute-done.20.refs_1_, bf16[32,3072]{1,0:T(8,128)(2,1)S(1)} %collective-permute-done.21.refs_2_, ...), custom_call_target="tpu_custom_call" | custom-call | flops 104857600 | bytes 4194304 | tf_op jit(solution)/shard_map/pallas_call | solution.py:323
  (26 shorter events, 0.1 us)
Async XLA Ops:
  1.4 1.1 copy-start.2
  2.5 0.7 copy-start.4
  4.3 21.3 %collective-permute-start.6 = (bf16[96,4096]{1,0:T(8,128)(2,1)S(1)}, bf16[96,4096]{1,0:T(8,128)(2,1)S(1)}, u32[]{:S(2)}, u32[]{:S(2)}) collective-permute-start(bf16[96,4096]{1,0:T(8,128)(2,1)S(1)} %get-tuple-element.17.refs_0_), channel_id=1, source_target_pairs={{0,1},{1,0},{2,3},{3,2},{4,5},{5,4},{6,7},{7,6},{8,9},{9,8},{10,11... | collective-permute-start | bytes 2359304 | tf_op jit(solution)/shard_map/ppermute | solution.py:417
  4.8 9.7 %collective-permute-start = (bf16[32,4096]{1,0:T(8,128)(2,1)S(1)}, bf16[32,4096]{1,0:T(8,128)(2,1)S(1)}, u32[]{:S(2)}, u32[]{:S(2)}) collective-permute-start(bf16[32,4096]{1,0:T(8,128)(2,1)S(1)} %get-tuple-element.14), channel_id=1, source_target_pairs={{0,2},{2,0},{1,3},{3,1},{4,6},{6,4},{5,7},{7,5},{8,10},{10,8},{9,1... | collective-permute-start | bytes 786440 | tf_op jit(solution)/shard_map/ppermute | solution.py:420
  7.4 12.8 %collective-permute-start.1 = (bf16[32,4096]{1,0:T(8,128)(2,1)S(1)}, bf16[32,4096]{1,0:T(8,128)(2,1)S(1)}, u32[]{:S(2)}, u32[]{:S(2)}) collective-permute-start(bf16[32,4096]{1,0:T(8,128)(2,1)S(1)} %get-tuple-element.15), channel_id=1, source_target_pairs={{0,2},{2,0},{1,3},{3,1},{4,6},{6,4},{5,7},{7,5},{8,10},{10,8},{9,1... | collective-permute-start | bytes 786440 | tf_op jit(solution)/shard_map/ppermute | solution.py:420
  7.5 18.1 %collective-permute-start.2 = (bf16[32,4096]{1,0:T(8,128)(2,1)S(1)}, bf16[32,4096]{1,0:T(8,128)(2,1)S(1)}, u32[]{:S(2)}, u32[]{:S(2)}) collective-permute-start(bf16[32,4096]{1,0:T(8,128)(2,1)S(1)} %get-tuple-element.16), channel_id=1, source_target_pairs={{0,2},{2,0},{1,3},{3,1},{4,6},{6,4},{5,7},{7,5},{8,10},{10,8},{9,1... | collective-permute-start | bytes 786440 | tf_op jit(solution)/shard_map/ppermute | solution.py:420
  14.5 24.9 %collective-permute-start.3 = (bf16[32,4096]{1,0:T(8,128)(2,1)S(1)}, bf16[32,4096]{1,0:T(8,128)(2,1)S(1)}, u32[]{:S(2)}, u32[]{:S(2)}) collective-permute-start(bf16[32,4096]{1,0:T(8,128)(2,1)S(1)} %collective-permute-done.refs_0_), channel_id=1, source_target_pairs={{0,1},{1,0},{2,3},{3,2},{4,5},{5,4},{6,7},{7,6},{8,9},{9,8},{10,11... | collective-permute-start | bytes 786440 | tf_op jit(solution)/shard_map/ppermute | solution.py:417
  20.2 19.3 %collective-permute-start.4 = (bf16[32,4096]{1,0:T(8,128)(2,1)S(1)}, bf16[32,4096]{1,0:T(8,128)(2,1)S(1)}, u32[]{:S(2)}, u32[]{:S(2)}) collective-permute-start(bf16[32,4096]{1,0:T(8,128)(2,1)S(1)} %collective-permute-done.1.refs_1_), channel_id=1, source_target_pairs={{0,1},{1,0},{2,3},{3,2},{4,5},{5,4},{6,7},{7,6},{8,9},{9,8},{10,11... | collective-permute-start | bytes 786440 | tf_op jit(solution)/shard_map/ppermute | solution.py:417
  25.5 13.9 %collective-permute-start.5 = (bf16[32,4096]{1,0:T(8,128)(2,1)S(1)}, bf16[32,4096]{1,0:T(8,128)(2,1)S(1)}, u32[]{:S(2)}, u32[]{:S(2)}) collective-permute-start(bf16[32,4096]{1,0:T(8,128)(2,1)S(1)} %collective-permute-done.2.refs_2_), channel_id=1, source_target_pairs={{0,1},{1,0},{2,3},{3,2},{4,5},{5,4},{6,7},{7,6},{8,9},{9,8},{10,11... | collective-permute-start | bytes 786440 | tf_op jit(solution)/shard_map/ppermute | solution.py:417
  25.5 1.2 copy-start
  26.8 0.7 copy-start.5
  27.5 12.0 %copy-start.1 = (bf16[128,4096]{1,0:T(8,128)(2,1)S(1)}, bf16[128,4096]{1,0:T(8,128)(2,1)}, u32[]{:S(2)}) copy-start(bf16[128,4096]{1,0:T(8,128)(2,1)} %target_ref.7) | copy-start | bytes 3145732
  63.0 6.8 %collective-permute-start.13 = (bf16[192,1024]{1,0:T(8,128)(2,1)S(1)}, bf16[192,1024]{1,0:T(8,128)(2,1)S(1)}, u32[]{:S(2)}, u32[]{:S(2)}) collective-permute-start(bf16[192,1024]{1,0:T(8,128)(2,1)S(1)} %get-tuple-element.23), channel_id=1, source_target_pairs={{0,1},{1,0},{2,3},{3,2},{4,5},{5,4},{6,7},{7,6},{8,9},{9,8},{10,11... | collective-permute-start | bytes 1179656 | tf_op jit(solution)/shard_map/ppermute | solution.py:417
  63.6 8.7 %collective-permute-start.10 = (bf16[192,1024]{1,0:T(8,128)(2,1)S(1)}, bf16[192,1024]{1,0:T(8,128)(2,1)S(1)}, u32[]{:S(2)}, u32[]{:S(2)}) collective-permute-start(bf16[192,1024]{1,0:T(8,128)(2,1)S(1)} %get-tuple-element.21), channel_id=1, source_target_pairs={{0,1},{1,0},{2,3},{3,2},{4,5},{5,4},{6,7},{7,6},{8,9},{9,8},{10,11... | collective-permute-start | bytes 1179656 | tf_op jit(solution)/shard_map/ppermute | solution.py:417
  66.4 6.8 %collective-permute-start.7 = (bf16[192,1024]{1,0:T(8,128)(2,1)S(1)}, bf16[192,1024]{1,0:T(8,128)(2,1)S(1)}, u32[]{:S(2)}, u32[]{:S(2)}) collective-permute-start(bf16[192,1024]{1,0:T(8,128)(2,1)S(1)} %get-tuple-element.19), channel_id=1, source_target_pairs={{0,1},{1,0},{2,3},{3,2},{4,5},{5,4},{6,7},{7,6},{8,9},{9,8},{10,11... | collective-permute-start | bytes 1179656 | tf_op jit(solution)/shard_map/ppermute | solution.py:417
  69.7 9.4 %copy-start.3 = (bf16[96,4096]{1,0:T(8,128)(2,1)S(1)}, bf16[96,4096]{1,0:T(8,128)(2,1)}, u32[]{:S(2)}) copy-start(bf16[96,4096]{1,0:T(8,128)(2,1)} %source_ref.7) | copy-start | bytes 2359300
  69.7 18.9 %collective-permute-start.16 = (bf16[192,1024]{1,0:T(8,128)(2,1)S(1)}, bf16[192,1024]{1,0:T(8,128)(2,1)S(1)}, u32[]{:S(2)}, u32[]{:S(2)}) collective-permute-start(bf16[192,1024]{1,0:T(8,128)(2,1)S(1)} %get-tuple-element.25), channel_id=1, source_target_pairs={{0,1},{1,0},{2,3},{3,2},{4,5},{5,4},{6,7},{7,6},{8,9},{9,8},{10,11... | collective-permute-start | bytes 1179656 | tf_op jit(solution)/shard_map/ppermute | solution.py:417
  70.5 8.7 %collective-permute-start.14 = (bf16[96,1024]{1,0:T(8,128)(2,1)S(1)}, bf16[96,1024]{1,0:T(8,128)(2,1)S(1)}, u32[]{:S(2)}, u32[]{:S(2)}) collective-permute-start(bf16[96,1024]{1,0:T(8,128)(2,1)S(1)} %shard_map.72), channel_id=1, source_target_pairs={{0,2},{2,0},{1,3},{3,1},{4,6},{6,4},{5,7},{7,5},{8,10},{10,8},{9,1... | collective-permute-start | bytes 589832 | tf_op jit(solution)/shard_map/ppermute | solution.py:420
  72.9 9.6 %collective-permute-start.11 = (bf16[96,1024]{1,0:T(8,128)(2,1)S(1)}, bf16[96,1024]{1,0:T(8,128)(2,1)S(1)}, u32[]{:S(2)}, u32[]{:S(2)}) collective-permute-start(bf16[96,1024]{1,0:T(8,128)(2,1)S(1)} %shard_map.70), channel_id=1, source_target_pairs={{0,2},{2,0},{1,3},{3,1},{4,6},{6,4},{5,7},{7,5},{8,10},{10,8},{9,1... | collective-permute-start | bytes 589832 | tf_op jit(solution)/shard_map/ppermute | solution.py:420
  73.8 12.4 %collective-permute-start.8 = (bf16[96,1024]{1,0:T(8,128)(2,1)S(1)}, bf16[96,1024]{1,0:T(8,128)(2,1)S(1)}, u32[]{:S(2)}, u32[]{:S(2)}) collective-permute-start(bf16[96,1024]{1,0:T(8,128)(2,1)S(1)} %shard_map.68), channel_id=1, source_target_pairs={{0,2},{2,0},{1,3},{3,1},{4,6},{6,4},{5,7},{7,5},{8,10},{10,8},{9,1... | collective-permute-start | bytes 589832 | tf_op jit(solution)/shard_map/ppermute | solution.py:420
  75.6 53.7 %collective-permute-start.26 = (bf16[128,4096]{1,0:T(8,128)(2,1)S(1)}, bf16[128,4096]{1,0:T(8,128)(2,1)S(1)}, u32[]{:S(2)}, u32[]{:S(2)}) collective-permute-start(bf16[128,4096]{1,0:T(8,128)(2,1)S(1)} %copy-done.1), channel_id=1, source_target_pairs={{0,4},{4,8},{8,12},{12,16},{1,5},{5,9},{9,13},{13,17},{2,6},{6,10}... | collective-permute-start | bytes 3145736 | tf_op jit(solution)/shard_map/ppermute | solution.py:424
  79.8 27.0 %collective-permute-start.15 = (bf16[96,1024]{1,0:T(8,128)(2,1)S(1)}, bf16[96,1024]{1,0:T(8,128)(2,1)S(1)}, u32[]{:S(2)}, u32[]{:S(2)}) collective-permute-start(bf16[96,1024]{1,0:T(8,128)(2,1)S(1)} %shard_map.73), channel_id=1, source_target_pairs={{0,4},{4,8},{8,12},{12,16},{16,20},{20,24},{24,28},{28,0},{1,5},{5... | collective-permute-start | bytes 589832 | tf_op jit(solution)/shard_map/ppermute | solution.py:424
  83.2 27.8 %collective-permute-start.12 = (bf16[96,1024]{1,0:T(8,128)(2,1)S(1)}, bf16[96,1024]{1,0:T(8,128)(2,1)S(1)}, u32[]{:S(2)}, u32[]{:S(2)}) collective-permute-start(bf16[96,1024]{1,0:T(8,128)(2,1)S(1)} %shard_map.71), channel_id=1, source_target_pairs={{0,4},{4,8},{8,12},{12,16},{16,20},{20,24},{24,28},{28,0},{1,5},{5... | collective-permute-start | bytes 589832 | tf_op jit(solution)/shard_map/ppermute | solution.py:424
  86.9 27.0 %collective-permute-start.9 = (bf16[96,1024]{1,0:T(8,128)(2,1)S(1)}, bf16[96,1024]{1,0:T(8,128)(2,1)S(1)}, u32[]{:S(2)}, u32[]{:S(2)}) collective-permute-start(bf16[96,1024]{1,0:T(8,128)(2,1)S(1)} %shard_map.69), channel_id=1, source_target_pairs={{0,4},{4,8},{8,12},{12,16},{16,20},{20,24},{24,28},{28,0},{1,5},{5... | collective-permute-start | bytes 589832 | tf_op jit(solution)/shard_map/ppermute | solution.py:424
  88.7 36.4 %collective-permute-start.19 = (bf16[96,4096]{1,0:T(8,128)(2,1)S(1)}, bf16[96,4096]{1,0:T(8,128)(2,1)S(1)}, u32[]{:S(2)}, u32[]{:S(2)}) collective-permute-start(bf16[96,4096]{1,0:T(8,128)(2,1)S(1)} %copy-done.3), channel_id=1, source_target_pairs={{16,20},{20,24},{24,28},{28,0},{17,21},{21,25},{25,29},{29,1},{18,... | collective-permute-start | bytes 2359304 | tf_op jit(solution)/shard_map/ppermute | solution.py:424
  106.8 7.7 %collective-permute-start.17 = (bf16[96,1024]{1,0:T(8,128)(2,1)S(1)}, bf16[96,1024]{1,0:T(8,128)(2,1)S(1)}, u32[]{:S(2)}, u32[]{:S(2)}) collective-permute-start(bf16[96,1024]{1,0:T(8,128)(2,1)S(1)} %shard_map.74), channel_id=1, source_target_pairs={{0,2},{2,0},{1,3},{3,1},{4,6},{6,4},{5,7},{7,5},{8,10},{10,8},{9,1... | collective-permute-start | bytes 589832 | tf_op jit(solution)/shard_map/ppermute | solution.py:420
  113.9 5.7 %collective-permute-start.21 = (bf16[32,3072]{1,0:T(8,128)(2,1)S(1)}, bf16[32,3072]{1,0:T(8,128)(2,1)S(1)}, u32[]{:S(2)}, u32[]{:S(2)}) collective-permute-start(bf16[32,3072]{1,0:T(8,128)(2,1)S(1)} %pad_maximum_fusion.refs_0_), channel_id=1, source_target_pairs={{0,2},{2,0},{1,3},{3,1},{4,6},{6,4},{5,7},{7,5},{8,10},{10,8},{9,1... | collective-permute-start | bytes 589832 | tf_op jit(solution)/shard_map/ppermute | solution.py:420
  115.1 8.4 %collective-permute-start.18 = (bf16[96,1024]{1,0:T(8,128)(2,1)S(1)}, bf16[96,1024]{1,0:T(8,128)(2,1)S(1)}, u32[]{:S(2)}, u32[]{:S(2)}) collective-permute-start(bf16[96,1024]{1,0:T(8,128)(2,1)S(1)} %shard_map.75), channel_id=1, source_target_pairs={{0,4},{4,8},{8,12},{12,16},{16,20},{20,24},{24,28},{28,0},{1,5},{5... | collective-permute-start | bytes 589832 | tf_op jit(solution)/shard_map/ppermute | solution.py:424
  117.7 11.7 %collective-permute-start.20 = (bf16[32,3072]{1,0:T(8,128)(2,1)S(1)}, bf16[32,3072]{1,0:T(8,128)(2,1)S(1)}, u32[]{:S(2)}, u32[]{:S(2)}) collective-permute-start(bf16[32,3072]{1,0:T(8,128)(2,1)S(1)} %pad_maximum_fusion.refs_0_), channel_id=1, source_target_pairs={{0,1},{1,0},{2,3},{3,2},{4,5},{5,4},{6,7},{7,6},{8,9},{9,8},{10,11... | collective-permute-start | bytes 589832 | tf_op jit(solution)/shard_map/ppermute | solution.py:417
  119.6 9.7 %collective-permute-start.22 = (bf16[32,3072]{1,0:T(8,128)(2,1)S(1)}, bf16[32,3072]{1,0:T(8,128)(2,1)S(1)}, u32[]{:S(2)}, u32[]{:S(2)}) collective-permute-start(bf16[32,3072]{1,0:T(8,128)(2,1)S(1)} %collective-permute-done.21.refs_2_), channel_id=1, source_target_pairs={{0,1},{1,0},{2,3},{3,2},{4,5},{5,4},{6,7},{7,6},{8,9},{9,8},{10,11... | collective-permute-start | bytes 589832 | tf_op jit(solution)/shard_map/ppermute | solution.py:417
  123.5 4.3 %collective-permute-start.24 = (bf16[32,1024]{1,0:T(8,128)(2,1)S(1)}, bf16[32,1024]{1,0:T(8,128)(2,1)S(1)}, u32[]{:S(2)}, u32[]{:S(2)}) collective-permute-start(bf16[32,1024]{1,0:T(8,128)(2,1)S(1)} %slice.19.refs_4_), channel_id=1, source_target_pairs={{0,2},{2,0},{1,3},{3,1},{4,6},{6,4},{5,7},{7,5},{8,10},{10,8},{9,1... | collective-permute-start | bytes 196616 | tf_op jit(solution)/shard_map/ppermute | solution.py:420
  125.1 4.3 %collective-permute-start.23 = (bf16[32,1024]{1,0:T(8,128)(2,1)S(1)}, bf16[32,1024]{1,0:T(8,128)(2,1)S(1)}, u32[]{:S(2)}, u32[]{:S(2)}) collective-permute-start(bf16[32,1024]{1,0:T(8,128)(2,1)S(1)} %slice.19.refs_4_), channel_id=1, source_target_pairs={{0,1},{1,0},{2,3},{3,2},{4,5},{5,4},{6,7},{7,6},{8,9},{9,8},{10,11... | collective-permute-start | bytes 196616 | tf_op jit(solution)/shard_map/ppermute | solution.py:417
  127.8 1.5 %collective-permute-start.25 = (bf16[32,1024]{1,0:T(8,128)(2,1)S(1)}, bf16[32,1024]{1,0:T(8,128)(2,1)S(1)}, u32[]{:S(2)}, u32[]{:S(2)}) collective-permute-start(bf16[32,1024]{1,0:T(8,128)(2,1)S(1)} %collective-permute-done.24.refs_6_), channel_id=1, source_target_pairs={{0,1},{1,0},{2,3},{3,2},{4,5},{5,4},{6,7},{7,6},{8,9},{9,8},{10,11... | collective-permute-start | bytes 196616 | tf_op jit(solution)/shard_map/ppermute | solution.py:417
where the time goes:
time: 132 us; the launch traced here: 131 us
  Pallas kernels  50 us (38%)
  waiting for transfers between devices  50 us (38%)
  starting transfers between devices  25.5 us (19%)
  local copies, waits for them, and re-layouts  3.91 us (3%)
  between operations  1.55 us (1%)
    ppermute x6, waiting for transfers between devices, onward(): return lax.ppermute(value, 'section', pairs)  26.7 us
    pallas_call x2, Pallas kernels, qkv_rows(): pl.pallas_call(functools.partial(qkv_kernel, n_pieces, per), grid_spec=pl...  23.9 us
    ppermute x9, waiting for transfers between devices, across(): return lax.ppermute(value, 'fsdp', [(0, 2), (2, 0), (1, 3), (3, 1)])  23.3 us
    ppermute x6, starting transfers between devices, onward(): return lax.ppermute(value, 'section', pairs)  12.4 us
    ppermute x9, starting transfers between devices, across(): return lax.ppermute(value, 'fsdp', [(0, 2), (2, 0), (1, 3), (3, 1)])  11.2 us
    pallas_call x4, Pallas kernels, out_chunk(): pl.pallas_call(out_kernel, grid_spec=pltpu.PrefetchScalarGridSpec(num_sca...  11 us
    pallas_call x10, Pallas kernels, small_call(): pl.pallas_call(kernel, grid_spec=pltpu.PrefetchScalarGridSpec(num_scalar_...  7.98 us
    pallas_call x1, Pallas kernels, attend_rows(): pl.pallas_call(attend_kernel, grid_spec=pltpu.PrefetchScalarGridSpec(num_...  6.08 us
  transfers between devices with their start and end apart: 27, of which 11 were waited for; matrix products, arithmetic and copies ran while one was open for 0% of the time, Pallas kernels for 18%

commit v1 on v0

--- a/solution.py
+++ b/solution.py
@@ -273,15 +273,23 @@
     )(ids, qkv, qkv, qkv)
 
 
-def out_kernel(ids, c0, c1, c2, c3, w_ref, keep_ref, send_ref):
+def out_kernel(ids, c0, c1, c2, c3, w_ref, source_ref, target_ref, base_ref, keep_ref, send_ref):
     context = jnp.concatenate([c[...] for c in (c0, c1, c2, c3)], axis=0)
     terms = out_partial(context, w_ref[...]).astype(jnp.bfloat16)
     half = terms.shape[0] // 2
-    keep_ref[...] = terms[:half]
+    own = half // 2
+    mine = terms[:own].astype(jnp.float32)
+    base_ref[...] = source_ref[...].astype(jnp.float32) + mine
+    keep_ref[...] = terms[own:half]
     send_ref[...] = terms[half:]
 
-
-def out_chunk(ids, context, attn_weights, chunk, parts):
+    @pl.when(ids[0] == 0)
+    def _():
+        part = target_ref.shape[0]
+        base_ref[0:part, :] = target_ref[...].astype(jnp.float32) + mine[:part]
+
+
+def out_chunk(ids, context, attn_weights, source_rows, target_rows, chunk, parts):
     total, inner = context.shape
     span = attn_weights.shape[2] // parts
     tile = span // 2
@@ -301,24 +309,31 @@
                 rows_spec(7),
                 rows_spec(8),
                 pl.BlockSpec((None, None, tile, inner), lambda i, s: (0, 3, 2 * chunk + i, 0)),
+                pl.BlockSpec((total // 4, tile), lambda i, s: (0, 2 * chunk + i)),
+                pl.BlockSpec((target_rows.shape[0] // 4, tile), lambda i, s: (s[5], 2 * chunk + i)),
             ],
-            out_specs=[pl.BlockSpec((total // 2, tile), lambda i, s: (0, i))] * 2,
-        ),
-        out_shape=[half, half],
+            out_specs=[
+                pl.BlockSpec((total // 4, tile), lambda i, s: (0, i)),
+                pl.BlockSpec((total // 4, tile), lambda i, s: (0, i)),
+                pl.BlockSpec((total // 2, tile), lambda i, s: (0, i)),
+            ],
+        ),
+        out_shape=[
+            jax.ShapeDtypeStruct((total // 4, span), jnp.float32),
+            jax.ShapeDtypeStruct((total // 4, span), jnp.bfloat16),
+            half,
+        ],
         compiler_params=WEIGHT_PARAMS,
         cost_estimate=pl.CostEstimate(
             flops=2 * total * span * inner, bytes_accessed=2 * span * inner, transcendentals=0
         ),
         name="out_chunk",
-    )(ids, context, context, context, context, attn_weights)
+    )(ids, context, context, context, context, attn_weights, source_rows, target_rows)
 
 
 def small_call(kernel, ids, operands, blocks, out_shape):
     def spec(shape, index):
-        row, column = index
-        if row == "here":
-            return pl.BlockSpec(shape, lambda i, s: (s[5], column))
-        return pl.BlockSpec(shape, lambda i, s: (row, column))
+        return pl.BlockSpec(shape, lambda i, s: index)
 
     return pl.pallas_call(
         kernel,
@@ -344,15 +359,10 @@
     ).astype(jnp.bfloat16)
 
 
-def final_kernel(ids, keep_ref, taken_ref, crossed_ref, source_ref, target_ref, o_ref):
+def final_kernel(ids, base_ref, taken_ref, crossed_ref, o_ref):
     f32 = jnp.float32
-    total = keep_ref[...].astype(f32) + taken_ref[...].astype(f32) + crossed_ref[...].astype(f32)
-    o_ref[...] = (source_ref[...].astype(f32) + total).astype(jnp.bfloat16)
-
-    @pl.when(ids[0] == 0)
-    def _():
-        part = target_ref.shape[0]
-        o_ref[0:part, :] = (target_ref[...].astype(f32) + total[:part]).astype(jnp.bfloat16)
+    total = base_ref[...] + taken_ref[...].astype(f32) + crossed_ref[...].astype(f32)
+    o_ref[...] = total.astype(jnp.bfloat16)
 
 
 def target_kernel(ids, *refs):
@@ -442,18 +452,16 @@
     block = (own, span)
     moved = []
     for i in range(PARTS):
-        keep, send = out_chunk(ids, context, attn_weights, i, PARTS)
+        base, keep, send = out_chunk(ids, context, attn_weights, source_rows, target_rows, i, PARTS)
         taken = to_sibling(send)
         for_other = small_call(
             pair_kernel, ids,
-            [keep, taken], [(block, (1, 0)), (block, (1, 0))], block,
+            [keep, taken], [(block, (0, 0)), (block, (1, 0))], block,
         )
         crossed = across(for_other)
         new = small_call(
             final_kernel, ids,
-            [keep, taken, crossed, source_rows, target_rows],
-            [(block, (0, 0))] * 3 + [(block, (0, i)), ((part, span), ("here", i))],
-            block,
+            [base, taken, crossed], [(block, (0, 0))] * 3, block,
         )
         moved.append(onward(new, 0, n_section))
 

time: 132 us -> 132 us (level)
  no operation moved by 1% of the time
where the time goes in v1:
time: 132 us; the launch traced here: 131 us
  Pallas kernels  50.2 us (38%)
  waiting for transfers between devices  50.1 us (38%)
  starting transfers between devices  25.5 us (19%)
  local copies, waits for them, and re-layouts  3.91 us (3%)
  between operations  1.55 us (1%)
    ppermute x6, waiting for transfers between devices, onward(): return lax.ppermute(value, 'section', pairs)  26.7 us
    pallas_call x2, Pallas kernels, qkv_rows(): pl.pallas_call(functools.partial(qkv_kernel, n_pieces, per), grid_spec=pl...  23.9 us
    ppermute x9, waiting for transfers between devices, across(): return lax.ppermute(value, 'fsdp', [(0, 2), (2, 0), (1, 3), (3, 1)])  23.4 us
    ppermute x6, starting transfers between devices, onward(): return lax.ppermute(value, 'section', pairs)  12.4 us
    pallas_call x4, Pallas kernels, out_chunk(): pl.pallas_call(out_kernel, grid_spec=pltpu.PrefetchScalarGridSpec(num_sca...  11.4 us
    ppermute x9, starting transfers between devices, across(): return lax.ppermute(value, 'fsdp', [(0, 2), (2, 0), (1, 3), (3, 1)])  11.2 us
    pallas_call x10, Pallas kernels, small_call(): pl.pallas_call(kernel, grid_spec=pltpu.PrefetchScalarGridSpec(num_scalar_...  7.83 us
    pallas_call x1, Pallas kernels, attend_rows(): pl.pallas_call(attend_kernel, grid_spec=pltpu.PrefetchScalarGridSpec(num_...  6.09 us
  transfers between devices with their start and end apart: 27, of which 11 were waited for; matrix products, arithmetic and copies ran while one was open for 0% of the time, Pallas kernels for 18%

profile of v1, /device:TPU:0, one launch (start us, length us, event | category | flops | bytes accessed | tf_op | source)
XLA Modules:
  0.0 131.2 jit_solution(1377891592470566235)
XLA Ops:
  1.3 0.1 stack.47.ids
  1.4 1.1 copy-done.2
  2.5 0.7 copy-done.4
  3.2 1.0 norm_rows.1
  4.3 0.6 collective-permute-start.6
  4.8 2.6 %collective-permute-start = (bf16[32,4096]{1,0:T(8,128)(2,1)S(1)}, bf16[32,4096]{1,0:T(8,128)(2,1)S(1)}, u32[]{:S(2)}, u32[]{:S(2)}) collective-permute-start(bf16[32,4096]{1,0:T(8,128)(2,1)S(1)} %get-tuple-element.18), channel_id=1, source_target_pairs={{0,2},{2,0},{1,3},{3,1},{4,6},{6,4},{5,7},{7,5},{8,10},{10,8},{9,1... | collective-permute-start | bytes 786440 | tf_op jit(solution)/shard_map/ppermute | solution.py:430
  7.4 0.1 collective-permute-start.1
  7.5 1.9 %collective-permute-start.2 = (bf16[32,4096]{1,0:T(8,128)(2,1)S(1)}, bf16[32,4096]{1,0:T(8,128)(2,1)S(1)}, u32[]{:S(2)}, u32[]{:S(2)}) collective-permute-start(bf16[32,4096]{1,0:T(8,128)(2,1)S(1)} %get-tuple-element.20), channel_id=1, source_target_pairs={{0,2},{2,0},{1,3},{3,1},{4,6},{6,4},{5,7},{7,5},{8,10},{10,8},{9,1... | collective-permute-start | bytes 786440 | tf_op jit(solution)/shard_map/ppermute | solution.py:430
  9.4 5.1 %collective-permute-done.refs_0_ = bf16[32,4096]{1,0:T(8,128)(2,1)S(1)} collective-permute-done((bf16[32,4096]{1,0:T(8,128)(2,1)S(1)}, bf16[32,4096]{1,0:T(8,128)(2,1)S(1)}, u32[]{:S(2)}, u32[]{:S(2)}) %collective-permute-start) | collective-permute-done | bytes 262176 | tf_op jit(solution)/shard_map/ppermute | solution.py:430
  14.6 5.6 %collective-permute-done.1.refs_1_ = bf16[32,4096]{1,0:T(8,128)(2,1)S(1)} collective-permute-done((bf16[32,4096]{1,0:T(8,128)(2,1)S(1)}, bf16[32,4096]{1,0:T(8,128)(2,1)S(1)}, u32[]{:S(2)}, u32[]{:S(2)}) %collective-permute-start.1) | collective-permute-done | bytes 262176 | tf_op jit(solution)/shard_map/ppermute | solution.py:430
  20.2 5.4 %collective-permute-done.2.refs_2_ = bf16[32,4096]{1,0:T(8,128)(2,1)S(1)} collective-permute-done((bf16[32,4096]{1,0:T(8,128)(2,1)S(1)}, bf16[32,4096]{1,0:T(8,128)(2,1)S(1)}, u32[]{:S(2)}, u32[]{:S(2)}) %collective-permute-start.2) | collective-permute-done | bytes 262176 | tf_op jit(solution)/shard_map/ppermute | solution.py:430
  25.5 0.0 collective-permute-start.5
  25.5 0.0 collective-permute-done.6.refs_1_
  25.5 1.2 copy-done
  26.8 0.7 copy-done.5
  27.5 11.9 %qkv_rows.2.refs_9_ = bf16[384,2304]{1,0:T(8,128)(2,1)S(1)} custom-call(s32[10]{0:T(128)S(1)} %stack.47.ids, bf16[96,4096]{1,0:T(8,128)(2,1)S(1)} %get-tuple-element.21.refs_0_, bf16[96,4096]{1,0:T(8,128)(2,1)S(1)} %collective-permute-done.6.refs_1_, bf16[128,4096]{1,0:T(8,128)(2,1)S(1)} %copy-done, f32[1,4096]{1,0:T(1,128)S(1)} %copy-done.5, ...), custom_call_target="tpu_custom_call" | custom-call | flops 3623878656 | bytes 18874368 | tf_op jit(solution)/shard_map/qkv_rows/pallas_call | solution.py:202
  39.4 0.0 collective-permute-done.3.refs_3_
  39.4 0.0 collective-permute-done.4.refs_4_
  39.5 11.9 %qkv_rows.3.q_ref.k_ref.v_ref = bf16[384,2304]{1,0:T(8,128)(2,1)S(1)} custom-call(s32[10]{0:T(128)S(1)} %stack.47.ids, bf16[32,4096]{1,0:T(8,128)(2,1)S(1)} %collective-permute-done.refs_0_, bf16[32,4096]{1,0:T(8,128)(2,1)S(1)} %collective-permute-done.1.refs_1_, ...), custom_call_target="tpu_custom_call", output_to_operand_aliasing={{}: (10, {})} | custom-call | flops 3623878656 | bytes 18874368 | tf_op jit(solution)/shard_map/qkv_rows/pallas_call | solution.py:202
  51.4 0.0 copy-start.3
  51.4 6.1 %attend_rows.1.c0.c1.c2.c3 = bf16[384,768]{1,0:T(8,128)(2,1)S(1)} custom-call(s32[10]{0:T(128)S(1)} %stack.47.ids, bf16[384,2304]{1,0:T(8,128)(2,1)S(1)} %qkv_rows.3.q_ref.k_ref.v_ref, bf16[384,2304]{1,0:T(8,128)(2,1)S(1)} %qkv_rows.3.q_ref.k_ref.v_ref, bf16[384,2304]{1,0:T(8,128)(2,1)S(1)} %qkv_rows.3.q_ref.k_ref.v_ref), custom_call_target="tpu_custom_call" | custom-call | flops 4529848320 | bytes 2359296 | tf_op jit(solution)/shard_map/attend_rows/pallas_call | solution.py:255
  57.5 2.9 %out_chunk.6 = (f32[96,1024]{1,0:T(8,128)S(1)}, bf16[96,1024]{1,0:T(8,128)(2,1)S(1)}, bf16[192,1024]{1,0:T(8,128)(2,1)S(1)}) custom-call(s32[10]{0:T(128)S(1)} %stack.47.ids, bf16[384,768]{1,0:T(8,128)(2,1)S(1)} %attend_rows.1.c0.c1.c2.c3, bf16[384,768]{1,0:T(8,128)(2,1)S(1)} %attend_rows.1.c0.c1.c2.c3, bf16[384,768]{1,0:T(8,128)(2,1)S(1)} %attend_rows.1.c0.c1.c2.c3, ...), custom_call_target="tpu_custom_call" | custom-call | flops 603979776 | bytes 1572864 | tf_op jit(solution)/shard_map/out_chunk/pallas_call | solution.py:301
  60.4 2.8 %out_chunk.5 = (f32[96,1024]{1,0:T(8,128)S(1)}, bf16[96,1024]{1,0:T(8,128)(2,1)S(1)}, bf16[192,1024]{1,0:T(8,128)(2,1)S(1)}) custom-call(s32[10]{0:T(128)S(1)} %stack.47.ids, bf16[384,768]{1,0:T(8,128)(2,1)S(1)} %attend_rows.1.c0.c1.c2.c3, bf16[384,768]{1,0:T(8,128)(2,1)S(1)} %attend_rows.1.c0.c1.c2.c3, bf16[384,768]{1,0:T(8,128)(2,1)S(1)} %attend_rows.1.c0.c1.c2.c3, ...), custom_call_target="tpu_custom_call" | custom-call | flops 603979776 | bytes 1572864 | tf_op jit(solution)/shard_map/out_chunk/pallas_call | solution.py:301
  63.2 0.6 collective-permute-start.13
  63.8 0.1 collective-permute-start.10
  63.9 2.8 %out_chunk.4 = (f32[96,1024]{1,0:T(8,128)S(1)}, bf16[96,1024]{1,0:T(8,128)(2,1)S(1)}, bf16[192,1024]{1,0:T(8,128)(2,1)S(1)}) custom-call(s32[10]{0:T(128)S(1)} %stack.47.ids, bf16[384,768]{1,0:T(8,128)(2,1)S(1)} %attend_rows.1.c0.c1.c2.c3, bf16[384,768]{1,0:T(8,128)(2,1)S(1)} %attend_rows.1.c0.c1.c2.c3, bf16[384,768]{1,0:T(8,128)(2,1)S(1)} %attend_rows.1.c0.c1.c2.c3, ...), custom_call_target="tpu_custom_call" | custom-call | flops 603979776 | bytes 1572864 | tf_op jit(solution)/shard_map/out_chunk/pallas_call | solution.py:301
  66.7 0.5 collective-permute-start.7
  67.2 2.8 %out_chunk.7 = (f32[96,1024]{1,0:T(8,128)S(1)}, bf16[96,1024]{1,0:T(8,128)(2,1)S(1)}, bf16[192,1024]{1,0:T(8,128)(2,1)S(1)}) custom-call(s32[10]{0:T(128)S(1)} %stack.47.ids, bf16[384,768]{1,0:T(8,128)(2,1)S(1)} %attend_rows.1.c0.c1.c2.c3, bf16[384,768]{1,0:T(8,128)(2,1)S(1)} %attend_rows.1.c0.c1.c2.c3, bf16[384,768]{1,0:T(8,128)(2,1)S(1)} %attend_rows.1.c0.c1.c2.c3, ...), custom_call_target="tpu_custom_call" | custom-call | flops 603979776 | bytes 1572864 | tf_op jit(solution)/shard_map/out_chunk/pallas_call | solution.py:301
  70.1 0.1 collective-permute-start.16
  70.2 0.6 shard_map.72
  70.8 1.8 %collective-permute-start.14 = (bf16[96,1024]{1,0:T(8,128)(2,1)S(1)}, bf16[96,1024]{1,0:T(8,128)(2,1)S(1)}, u32[]{:S(2)}, u32[]{:S(2)}) collective-permute-start(bf16[96,1024]{1,0:T(8,128)(2,1)S(1)} %shard_map.72), channel_id=1, source_target_pairs={{0,2},{2,0},{1,3},{3,1},{4,6},{6,4},{5,7},{7,5},{8,10},{10,8},{9,1... | collective-permute-start | bytes 589832 | tf_op jit(solution)/shard_map/ppermute | solution.py:430
  72.6 0.0 collective-permute-done.10.taken_ref
  72.6 0.6 shard_map.70
  73.2 0.3 collective-permute-start.11
  73.6 0.0 collective-permute-done.7.taken_ref
  73.6 0.6 shard_map.68
  74.2 1.8 %collective-permute-start.8 = (bf16[96,1024]{1,0:T(8,128)(2,1)S(1)}, bf16[96,1024]{1,0:T(8,128)(2,1)S(1)}, u32[]{:S(2)}, u32[]{:S(2)}) collective-permute-start(bf16[96,1024]{1,0:T(8,128)(2,1)S(1)} %shard_map.68), channel_id=1, source_target_pairs={{0,2},{2,0},{1,3},{3,1},{4,6},{6,4},{5,7},{7,5},{8,10},{10,8},{9,1... | collective-permute-start | bytes 589832 | tf_op jit(solution)/shard_map/ppermute | solution.py:430
  76.0 3.5 %collective-permute-start.26 = (bf16[128,4096]{1,0:T(8,128)(2,1)S(1)}, bf16[128,4096]{1,0:T(8,128)(2,1)S(1)}, u32[]{:S(2)}, u32[]{:S(2)}) collective-permute-start(bf16[128,4096]{1,0:T(8,128)(2,1)S(1)} %copy-done.1), channel_id=1, source_target_pairs={{0,4},{4,8},{8,12},{12,16},{1,5},{5,9},{9,13},{13,17},{2,6},{6,10}... | collective-permute-start | bytes 3145736 | tf_op jit(solution)/shard_map/ppermute | solution.py:434
  79.5 0.6 shard_map.73
  80.1 1.5 %collective-permute-start.15 = (bf16[96,1024]{1,0:T(8,128)(2,1)S(1)}, bf16[96,1024]{1,0:T(8,128)(2,1)S(1)}, u32[]{:S(2)}, u32[]{:S(2)}) collective-permute-start(bf16[96,1024]{1,0:T(8,128)(2,1)S(1)} %shard_map.73), channel_id=1, source_target_pairs={{0,4},{4,8},{8,12},{12,16},{16,20},{20,24},{24,28},{28,0},{1,5},{5... | collective-permute-start | bytes 589832 | tf_op jit(solution)/shard_map/ppermute | solution.py:434
  81.6 1.3 collective-permute-done.11.crossed_ref
  82.9 0.6 shard_map.71
  83.5 1.8 %collective-permute-start.12 = (bf16[96,1024]{1,0:T(8,128)(2,1)S(1)}, bf16[96,1024]{1,0:T(8,128)(2,1)S(1)}, u32[]{:S(2)}, u32[]{:S(2)}) collective-permute-start(bf16[96,1024]{1,0:T(8,128)(2,1)S(1)} %shard_map.71), channel_id=1, source_target_pairs={{0,4},{4,8},{8,12},{12,16},{16,20},{20,24},{24,28},{28,0},{1,5},{5... | collective-permute-start | bytes 589832 | tf_op jit(solution)/shard_map/ppermute | solution.py:434
  85.3 1.3 collective-permute-done.8.crossed_ref
  86.5 0.6 shard_map.69
  87.2 1.8 %collective-permute-start.9 = (bf16[96,1024]{1,0:T(8,128)(2,1)S(1)}, bf16[96,1024]{1,0:T(8,128)(2,1)S(1)}, u32[]{:S(2)}, u32[]{:S(2)}) collective-permute-start(bf16[96,1024]{1,0:T(8,128)(2,1)S(1)} %shard_map.69), channel_id=1, source_target_pairs={{0,4},{4,8},{8,12},{12,16},{16,20},{20,24},{24,28},{28,0},{1,5},{5... | collective-permute-start | bytes 589832 | tf_op jit(solution)/shard_map/ppermute | solution.py:434
  89.0 1.3 collective-permute-start.19
  90.3 0.6 shard_map.74
  90.9 16.3 %collective-permute-done.15.refs_2_ = bf16[96,1024]{1,0:T(8,128)(2,1)S(1)} collective-permute-done((bf16[96,1024]{1,0:T(8,128)(2,1)S(1)}, bf16[96,1024]{1,0:T(8,128)(2,1)S(1)}, u32[]{:S(2)}, u32[]{:S(2)}) %collective-permute-start.15) | collective-permute-done | bytes 196640 | tf_op jit(solution)/shard_map/ppermute | solution.py:434
  107.1 0.5 collective-permute-start.17
  107.7 3.7 %collective-permute-done.12.refs_1_ = bf16[96,1024]{1,0:T(8,128)(2,1)S(1)} collective-permute-done((bf16[96,1024]{1,0:T(8,128)(2,1)S(1)}, bf16[96,1024]{1,0:T(8,128)(2,1)S(1)}, u32[]{:S(2)}, u32[]{:S(2)}) %collective-permute-start.12) | collective-permute-done | bytes 196640 | tf_op jit(solution)/shard_map/ppermute | solution.py:434
  111.4 2.8 %collective-permute-done.9.refs_0_ = bf16[96,1024]{1,0:T(8,128)(2,1)S(1)} collective-permute-done((bf16[96,1024]{1,0:T(8,128)(2,1)S(1)}, bf16[96,1024]{1,0:T(8,128)(2,1)S(1)}, u32[]{:S(2)}, u32[]{:S(2)}) %collective-permute-start.9) | collective-permute-done | bytes 196640 | tf_op jit(solution)/shard_map/ppermute | solution.py:434
  114.2 0.6 collective-permute-start.21
  114.8 0.0 collective-permute-done.17.crossed_ref
  114.8 0.6 shard_map.75
  115.4 2.5 %collective-permute-start.18 = (bf16[96,1024]{1,0:T(8,128)(2,1)S(1)}, bf16[96,1024]{1,0:T(8,128)(2,1)S(1)}, u32[]{:S(2)}, u32[]{:S(2)}) collective-permute-start(bf16[96,1024]{1,0:T(8,128)(2,1)S(1)} %shard_map.75), channel_id=1, source_target_pairs={{0,4},{4,8},{8,12},{12,16},{16,20},{20,24},{24,28},{28,0},{1,5},{5... | collective-permute-start | bytes 589832 | tf_op jit(solution)/shard_map/ppermute | solution.py:434
  118.0 0.0 collective-permute-start.20
  118.0 2.0 %collective-permute-done.21.refs_2_ = bf16[32,3072]{1,0:T(8,128)(2,1)S(1)} collective-permute-done((bf16[32,3072]{1,0:T(8,128)(2,1)S(1)}, bf16[32,3072]{1,0:T(8,128)(2,1)S(1)}, u32[]{:S(2)}, u32[]{:S(2)}) %collective-permute-start.21) | collective-permute-done | bytes 196640 | tf_op jit(solution)/shard_map/ppermute | solution.py:430
  120.0 0.0 collective-permute-start.22
  120.0 3.9 %collective-permute-done.18.refs_3_ = bf16[96,1024]{1,0:T(8,128)(2,1)S(1)} collective-permute-done((bf16[96,1024]{1,0:T(8,128)(2,1)S(1)}, bf16[96,1024]{1,0:T(8,128)(2,1)S(1)}, u32[]{:S(2)}, u32[]{:S(2)}) %collective-permute-start.18) | collective-permute-done | bytes 196640 | tf_op jit(solution)/shard_map/ppermute | solution.py:434
  123.9 1.5 %collective-permute-start.24 = (bf16[32,1024]{1,0:T(8,128)(2,1)S(1)}, bf16[32,1024]{1,0:T(8,128)(2,1)S(1)}, u32[]{:S(2)}, u32[]{:S(2)}) collective-permute-start(bf16[32,1024]{1,0:T(8,128)(2,1)S(1)} %slice.19.refs_4_), channel_id=1, source_target_pairs={{0,2},{2,0},{1,3},{3,1},{4,6},{6,4},{5,7},{7,5},{8,10},{10,8},{9,1... | collective-permute-start | bytes 196616 | tf_op jit(solution)/shard_map/ppermute | solution.py:430
  125.4 2.8 %collective-permute-done.24.refs_6_ = bf16[32,1024]{1,0:T(8,128)(2,1)S(1)} collective-permute-done((bf16[32,1024]{1,0:T(8,128)(2,1)S(1)}, bf16[32,1024]{1,0:T(8,128)(2,1)S(1)}, u32[]{:S(2)}, u32[]{:S(2)}) %collective-permute-start.24) | collective-permute-done | bytes 65568 | tf_op jit(solution)/shard_map/ppermute | solution.py:430
  128.1 1.5 %shard_map.76 = bf16[96,4096]{1,0:T(8,128)(2,1)} custom-call(s32[10]{0:T(128)S(1)} %stack.47.ids, bf16[96,1024]{1,0:T(8,128)(2,1)S(1)} %collective-permute-done.9.refs_0_, bf16[96,1024]{1,0:T(8,128)(2,1)S(1)} %collective-permute-done.12.refs_1_, bf16[96,1024]{1,0:T(8,128)(2,1)S(1)} %collective-permute-done.15.refs_2_, ...), custom_call_target="tpu_custom_call" | custom-call | flops 78643200 | bytes 3145728 | tf_op jit(solution)/shard_map/pallas_call | solution.py:338
  129.6 1.6 %shard_map.77 = bf16[128,4096]{1,0:T(8,128)(2,1)} custom-call(s32[10]{0:T(128)S(1)} %stack.47.ids, bf16[32,3072]{1,0:T(8,128)(2,1)S(1)} %pad_maximum_fusion.refs_0_, bf16[32,3072]{1,0:T(8,128)(2,1)S(1)} %collective-permute-done.20.refs_1_, bf16[32,3072]{1,0:T(8,128)(2,1)S(1)} %collective-permute-done.21.refs_2_, ...), custom_call_target="tpu_custom_call" | custom-call | flops 104857600 | bytes 4194304 | tf_op jit(solution)/shard_map/pallas_call | solution.py:338
  (26 shorter events, 0.1 us)
Async XLA Ops:
  1.4 1.1 copy-start.2
  2.5 0.7 copy-start.4
  4.3 21.3 %collective-permute-start.6 = (bf16[96,4096]{1,0:T(8,128)(2,1)S(1)}, bf16[96,4096]{1,0:T(8,128)(2,1)S(1)}, u32[]{:S(2)}, u32[]{:S(2)}) collective-permute-start(bf16[96,4096]{1,0:T(8,128)(2,1)S(1)} %get-tuple-element.21.refs_0_), channel_id=1, source_target_pairs={{0,1},{1,0},{2,3},{3,2},{4,5},{5,4},{6,7},{7,6},{8,9},{9,8},{10,11... | collective-permute-start | bytes 2359304 | tf_op jit(solution)/shard_map/ppermute | solution.py:427
  4.8 9.7 %collective-permute-start = (bf16[32,4096]{1,0:T(8,128)(2,1)S(1)}, bf16[32,4096]{1,0:T(8,128)(2,1)S(1)}, u32[]{:S(2)}, u32[]{:S(2)}) collective-permute-start(bf16[32,4096]{1,0:T(8,128)(2,1)S(1)} %get-tuple-element.18), channel_id=1, source_target_pairs={{0,2},{2,0},{1,3},{3,1},{4,6},{6,4},{5,7},{7,5},{8,10},{10,8},{9,1... | collective-permute-start | bytes 786440 | tf_op jit(solution)/shard_map/ppermute | solution.py:430
  7.4 12.8 %collective-permute-start.1 = (bf16[32,4096]{1,0:T(8,128)(2,1)S(1)}, bf16[32,4096]{1,0:T(8,128)(2,1)S(1)}, u32[]{:S(2)}, u32[]{:S(2)}) collective-permute-start(bf16[32,4096]{1,0:T(8,128)(2,1)S(1)} %get-tuple-element.19), channel_id=1, source_target_pairs={{0,2},{2,0},{1,3},{3,1},{4,6},{6,4},{5,7},{7,5},{8,10},{10,8},{9,1... | collective-permute-start | bytes 786440 | tf_op jit(solution)/shard_map/ppermute | solution.py:430
  7.5 18.1 %collective-permute-start.2 = (bf16[32,4096]{1,0:T(8,128)(2,1)S(1)}, bf16[32,4096]{1,0:T(8,128)(2,1)S(1)}, u32[]{:S(2)}, u32[]{:S(2)}) collective-permute-start(bf16[32,4096]{1,0:T(8,128)(2,1)S(1)} %get-tuple-element.20), channel_id=1, source_target_pairs={{0,2},{2,0},{1,3},{3,1},{4,6},{6,4},{5,7},{7,5},{8,10},{10,8},{9,1... | collective-permute-start | bytes 786440 | tf_op jit(solution)/shard_map/ppermute | solution.py:430
  14.5 24.9 %collective-permute-start.3 = (bf16[32,4096]{1,0:T(8,128)(2,1)S(1)}, bf16[32,4096]{1,0:T(8,128)(2,1)S(1)}, u32[]{:S(2)}, u32[]{:S(2)}) collective-permute-start(bf16[32,4096]{1,0:T(8,128)(2,1)S(1)} %collective-permute-done.refs_0_), channel_id=1, source_target_pairs={{0,1},{1,0},{2,3},{3,2},{4,5},{5,4},{6,7},{7,6},{8,9},{9,8},{10,11... | collective-permute-start | bytes 786440 | tf_op jit(solution)/shard_map/ppermute | solution.py:427
  20.2 19.3 %collective-permute-start.4 = (bf16[32,4096]{1,0:T(8,128)(2,1)S(1)}, bf16[32,4096]{1,0:T(8,128)(2,1)S(1)}, u32[]{:S(2)}, u32[]{:S(2)}) collective-permute-start(bf16[32,4096]{1,0:T(8,128)(2,1)S(1)} %collective-permute-done.1.refs_1_), channel_id=1, source_target_pairs={{0,1},{1,0},{2,3},{3,2},{4,5},{5,4},{6,7},{7,6},{8,9},{9,8},{10,11... | collective-permute-start | bytes 786440 | tf_op jit(solution)/shard_map/ppermute | solution.py:427
  25.5 13.9 %collective-permute-start.5 = (bf16[32,4096]{1,0:T(8,128)(2,1)S(1)}, bf16[32,4096]{1,0:T(8,128)(2,1)S(1)}, u32[]{:S(2)}, u32[]{:S(2)}) collective-permute-start(bf16[32,4096]{1,0:T(8,128)(2,1)S(1)} %collective-permute-done.2.refs_2_), channel_id=1, source_target_pairs={{0,1},{1,0},{2,3},{3,2},{4,5},{5,4},{6,7},{7,6},{8,9},{9,8},{10,11... | collective-permute-start | bytes 786440 | tf_op jit(solution)/shard_map/ppermute | solution.py:427
  25.5 1.2 copy-start
  26.8 0.7 copy-start.5
  27.5 12.0 %copy-start.1 = (bf16[128,4096]{1,0:T(8,128)(2,1)S(1)}, bf16[128,4096]{1,0:T(8,128)(2,1)}, u32[]{:S(2)}) copy-start(bf16[128,4096]{1,0:T(8,128)(2,1)} %target_ref.7) | copy-start | bytes 3145732
  51.4 6.1 %copy-start.3 = (bf16[96,4096]{1,0:T(8,128)(2,1)S(1)}, bf16[96,4096]{1,0:T(8,128)(2,1)}, u32[]{:S(2)}) copy-start(bf16[96,4096]{1,0:T(8,128)(2,1)} %source_ref.7) | copy-start | bytes 2359300
  63.2 7.0 %collective-permute-start.13 = (bf16[192,1024]{1,0:T(8,128)(2,1)S(1)}, bf16[192,1024]{1,0:T(8,128)(2,1)S(1)}, u32[]{:S(2)}, u32[]{:S(2)}) collective-permute-start(bf16[192,1024]{1,0:T(8,128)(2,1)S(1)} %get-tuple-element.29), channel_id=1, source_target_pairs={{0,1},{1,0},{2,3},{3,2},{4,5},{5,4},{6,7},{7,6},{8,9},{9,8},{10,11... | collective-permute-start | bytes 1179656 | tf_op jit(solution)/shard_map/ppermute | solution.py:427
  63.8 8.8 %collective-permute-start.10 = (bf16[192,1024]{1,0:T(8,128)(2,1)S(1)}, bf16[192,1024]{1,0:T(8,128)(2,1)S(1)}, u32[]{:S(2)}, u32[]{:S(2)}) collective-permute-start(bf16[192,1024]{1,0:T(8,128)(2,1)S(1)} %get-tuple-element.26), channel_id=1, source_target_pairs={{0,1},{1,0},{2,3},{3,2},{4,5},{5,4},{6,7},{7,6},{8,9},{9,8},{10,11... | collective-permute-start | bytes 1179656 | tf_op jit(solution)/shard_map/ppermute | solution.py:427
  66.7 6.8 %collective-permute-start.7 = (bf16[192,1024]{1,0:T(8,128)(2,1)S(1)}, bf16[192,1024]{1,0:T(8,128)(2,1)S(1)}, u32[]{:S(2)}, u32[]{:S(2)}) collective-permute-start(bf16[192,1024]{1,0:T(8,128)(2,1)S(1)} %get-tuple-element.23), channel_id=1, source_target_pairs={{0,1},{1,0},{2,3},{3,2},{4,5},{5,4},{6,7},{7,6},{8,9},{9,8},{10,11... | collective-permute-start | bytes 1179656 | tf_op jit(solution)/shard_map/ppermute | solution.py:427
  70.1 18.9 %collective-permute-start.16 = (bf16[192,1024]{1,0:T(8,128)(2,1)S(1)}, bf16[192,1024]{1,0:T(8,128)(2,1)S(1)}, u32[]{:S(2)}, u32[]{:S(2)}) collective-permute-start(bf16[192,1024]{1,0:T(8,128)(2,1)S(1)} %get-tuple-element.32), channel_id=1, source_target_pairs={{0,1},{1,0},{2,3},{3,2},{4,5},{5,4},{6,7},{7,6},{8,9},{9,8},{10,11... | collective-permute-start | bytes 1179656 | tf_op jit(solution)/shard_map/ppermute | solution.py:427
  70.8 8.7 %collective-permute-start.14 = (bf16[96,1024]{1,0:T(8,128)(2,1)S(1)}, bf16[96,1024]{1,0:T(8,128)(2,1)S(1)}, u32[]{:S(2)}, u32[]{:S(2)}) collective-permute-start(bf16[96,1024]{1,0:T(8,128)(2,1)S(1)} %shard_map.72), channel_id=1, source_target_pairs={{0,2},{2,0},{1,3},{3,1},{4,6},{6,4},{5,7},{7,5},{8,10},{10,8},{9,1... | collective-permute-start | bytes 589832 | tf_op jit(solution)/shard_map/ppermute | solution.py:430
  73.2 9.6 %collective-permute-start.11 = (bf16[96,1024]{1,0:T(8,128)(2,1)S(1)}, bf16[96,1024]{1,0:T(8,128)(2,1)S(1)}, u32[]{:S(2)}, u32[]{:S(2)}) collective-permute-start(bf16[96,1024]{1,0:T(8,128)(2,1)S(1)} %shard_map.70), channel_id=1, source_target_pairs={{0,2},{2,0},{1,3},{3,1},{4,6},{6,4},{5,7},{7,5},{8,10},{10,8},{9,1... | collective-permute-start | bytes 589832 | tf_op jit(solution)/shard_map/ppermute | solution.py:430
  74.2 12.4 %collective-permute-start.8 = (bf16[96,1024]{1,0:T(8,128)(2,1)S(1)}, bf16[96,1024]{1,0:T(8,128)(2,1)S(1)}, u32[]{:S(2)}, u32[]{:S(2)}) collective-permute-start(bf16[96,1024]{1,0:T(8,128)(2,1)S(1)} %shard_map.68), channel_id=1, source_target_pairs={{0,2},{2,0},{1,3},{3,1},{4,6},{6,4},{5,7},{7,5},{8,10},{10,8},{9,1... | collective-permute-start | bytes 589832 | tf_op jit(solution)/shard_map/ppermute | solution.py:430
  76.0 53.6 %collective-permute-start.26 = (bf16[128,4096]{1,0:T(8,128)(2,1)S(1)}, bf16[128,4096]{1,0:T(8,128)(2,1)S(1)}, u32[]{:S(2)}, u32[]{:S(2)}) collective-permute-start(bf16[128,4096]{1,0:T(8,128)(2,1)S(1)} %copy-done.1), channel_id=1, source_target_pairs={{0,4},{4,8},{8,12},{12,16},{1,5},{5,9},{9,13},{13,17},{2,6},{6,10}... | collective-permute-start | bytes 3145736 | tf_op jit(solution)/shard_map/ppermute | solution.py:434
  80.1 27.1 %collective-permute-start.15 = (bf16[96,1024]{1,0:T(8,128)(2,1)S(1)}, bf16[96,1024]{1,0:T(8,128)(2,1)S(1)}, u32[]{:S(2)}, u32[]{:S(2)}) collective-permute-start(bf16[96,1024]{1,0:T(8,128)(2,1)S(1)} %shard_map.73), channel_id=1, source_target_pairs={{0,4},{4,8},{8,12},{12,16},{16,20},{20,24},{24,28},{28,0},{1,5},{5... | collective-permute-start | bytes 589832 | tf_op jit(solution)/shard_map/ppermute | solution.py:434
  83.5 27.9 %collective-permute-start.12 = (bf16[96,1024]{1,0:T(8,128)(2,1)S(1)}, bf16[96,1024]{1,0:T(8,128)(2,1)S(1)}, u32[]{:S(2)}, u32[]{:S(2)}) collective-permute-start(bf16[96,1024]{1,0:T(8,128)(2,1)S(1)} %shard_map.71), channel_id=1, source_target_pairs={{0,4},{4,8},{8,12},{12,16},{16,20},{20,24},{24,28},{28,0},{1,5},{5... | collective-permute-start | bytes 589832 | tf_op jit(solution)/shard_map/ppermute | solution.py:434
  87.2 27.0 %collective-permute-start.9 = (bf16[96,1024]{1,0:T(8,128)(2,1)S(1)}, bf16[96,1024]{1,0:T(8,128)(2,1)S(1)}, u32[]{:S(2)}, u32[]{:S(2)}) collective-permute-start(bf16[96,1024]{1,0:T(8,128)(2,1)S(1)} %shard_map.69), channel_id=1, source_target_pairs={{0,4},{4,8},{8,12},{12,16},{16,20},{20,24},{24,28},{28,0},{1,5},{5... | collective-permute-start | bytes 589832 | tf_op jit(solution)/shard_map/ppermute | solution.py:434
  89.0 36.4 %collective-permute-start.19 = (bf16[96,4096]{1,0:T(8,128)(2,1)S(1)}, bf16[96,4096]{1,0:T(8,128)(2,1)S(1)}, u32[]{:S(2)}, u32[]{:S(2)}) collective-permute-start(bf16[96,4096]{1,0:T(8,128)(2,1)S(1)} %copy-done.3), channel_id=1, source_target_pairs={{16,20},{20,24},{24,28},{28,0},{17,21},{21,25},{25,29},{29,1},{18,... | collective-permute-start | bytes 2359304 | tf_op jit(solution)/shard_map/ppermute | solution.py:434
  107.1 7.7 %collective-permute-start.17 = (bf16[96,1024]{1,0:T(8,128)(2,1)S(1)}, bf16[96,1024]{1,0:T(8,128)(2,1)S(1)}, u32[]{:S(2)}, u32[]{:S(2)}) collective-permute-start(bf16[96,1024]{1,0:T(8,128)(2,1)S(1)} %shard_map.74), channel_id=1, source_target_pairs={{0,2},{2,0},{1,3},{3,1},{4,6},{6,4},{5,7},{7,5},{8,10},{10,8},{9,1... | collective-permute-start | bytes 589832 | tf_op jit(solution)/shard_map/ppermute | solution.py:430
  114.2 5.7 %collective-permute-start.21 = (bf16[32,3072]{1,0:T(8,128)(2,1)S(1)}, bf16[32,3072]{1,0:T(8,128)(2,1)S(1)}, u32[]{:S(2)}, u32[]{:S(2)}) collective-permute-start(bf16[32,3072]{1,0:T(8,128)(2,1)S(1)} %pad_maximum_fusion.refs_0_), channel_id=1, source_target_pairs={{0,2},{2,0},{1,3},{3,1},{4,6},{6,4},{5,7},{7,5},{8,10},{10,8},{9,1... | collective-permute-start | bytes 589832 | tf_op jit(solution)/shard_map/ppermute | solution.py:430
  115.4 8.4 %collective-permute-start.18 = (bf16[96,1024]{1,0:T(8,128)(2,1)S(1)}, bf16[96,1024]{1,0:T(8,128)(2,1)S(1)}, u32[]{:S(2)}, u32[]{:S(2)}) collective-permute-start(bf16[96,1024]{1,0:T(8,128)(2,1)S(1)} %shard_map.75), channel_id=1, source_target_pairs={{0,4},{4,8},{8,12},{12,16},{16,20},{20,24},{24,28},{28,0},{1,5},{5... | collective-permute-start | bytes 589832 | tf_op jit(solution)/shard_map/ppermute | solution.py:434
  118.0 11.7 %collective-permute-start.20 = (bf16[32,3072]{1,0:T(8,128)(2,1)S(1)}, bf16[32,3072]{1,0:T(8,128)(2,1)S(1)}, u32[]{:S(2)}, u32[]{:S(2)}) collective-permute-start(bf16[32,3072]{1,0:T(8,128)(2,1)S(1)} %pad_maximum_fusion.refs_0_), channel_id=1, source_target_pairs={{0,1},{1,0},{2,3},{3,2},{4,5},{5,4},{6,7},{7,6},{8,9},{9,8},{10,11... | collective-permute-start | bytes 589832 | tf_op jit(solution)/shard_map/ppermute | solution.py:427
  120.0 9.7 %collective-permute-start.22 = (bf16[32,3072]{1,0:T(8,128)(2,1)S(1)}, bf16[32,3072]{1,0:T(8,128)(2,1)S(1)}, u32[]{:S(2)}, u32[]{:S(2)}) collective-permute-start(bf16[32,3072]{1,0:T(8,128)(2,1)S(1)} %collective-permute-done.21.refs_2_), channel_id=1, source_target_pairs={{0,1},{1,0},{2,3},{3,2},{4,5},{5,4},{6,7},{7,6},{8,9},{9,8},{10,11... | collective-permute-start | bytes 589832 | tf_op jit(solution)/shard_map/ppermute | solution.py:427
  123.9 4.3 %collective-permute-start.24 = (bf16[32,1024]{1,0:T(8,128)(2,1)S(1)}, bf16[32,1024]{1,0:T(8,128)(2,1)S(1)}, u32[]{:S(2)}, u32[]{:S(2)}) collective-permute-start(bf16[32,1024]{1,0:T(8,128)(2,1)S(1)} %slice.19.refs_4_), channel_id=1, source_target_pairs={{0,2},{2,0},{1,3},{3,1},{4,6},{6,4},{5,7},{7,5},{8,10},{10,8},{9,1... | collective-permute-start | bytes 196616 | tf_op jit(solution)/shard_map/ppermute | solution.py:430
  125.4 4.3 %collective-permute-start.23 = (bf16[32,1024]{1,0:T(8,128)(2,1)S(1)}, bf16[32,1024]{1,0:T(8,128)(2,1)S(1)}, u32[]{:S(2)}, u32[]{:S(2)}) collective-permute-start(bf16[32,1024]{1,0:T(8,128)(2,1)S(1)} %slice.19.refs_4_), channel_id=1, source_target_pairs={{0,1},{1,0},{2,3},{3,2},{4,5},{5,4},{6,7},{7,6},{8,9},{9,8},{10,11... | collective-permute-start | bytes 196616 | tf_op jit(solution)/shard_map/ppermute | solution.py:427
  128.1 1.5 %collective-permute-start.25 = (bf16[32,1024]{1,0:T(8,128)(2,1)S(1)}, bf16[32,1024]{1,0:T(8,128)(2,1)S(1)}, u32[]{:S(2)}, u32[]{:S(2)}) collective-permute-start(bf16[32,1024]{1,0:T(8,128)(2,1)S(1)} %collective-permute-done.24.refs_6_), channel_id=1, source_target_pairs={{0,1},{1,0},{2,3},{3,2},{4,5},{5,4},{6,7},{7,6},{8,9},{9,8},{10,11... | collective-permute-start | bytes 196616 | tf_op jit(solution)/shard_map/ppermute | solution.py:427
